TPU v7x, 256 devices: a whole 4x4x8 slice. The times are simulated.
256 devices in a mesh: term: 16 (over z, y_hi), sec: 16 (over y_lo, x, core).
Axes of the slice: x: 4, y: 4 (y_hi: 2, y_lo: 2; y = y_hi * 2 + y_lo), z: 8, core: 2. Of those that a mesh axis runs over, the one named last changes fastest.
Arguments:
- state: bfloat16 [16, 768, 768], P('sec'), may hold values from -6 to 6
- left_environment: bfloat16 [16, 16, 768, 768], P('term', 'sec'), may hold values from -0.21875 to 0.21875
- right_environment: bfloat16 [16, 16, 768, 768], P('term', 'sec'), may hold values from -0.21875 to 0.21875
- site_blocks: bfloat16 [16, 768, 768], P('sec'), may hold values from -3 to 3
- sector_sizes: int32 [16], replicated, may hold values from 192 to 768, as said below
- term_shift: int32 [16], P('term'), may hold values from -1 to 1
Outputs:
- applied: float32 [16, 768, 768], P('sec', 'term')
- new_left: bfloat16 [16, 16, 768, 768], P('term', 'sec')
Inputs may be any that keep to these rules, and one draw needn't show every extreme that they name: `sector_sizes`: every sector holds at least 192 states and the largest sector holds exactly 768.
All inputs are finite; a program needn't handle non-finite values.
Results may differ from a plain program's by a relative error of at most 0.0049.
Values may be sent and summed in bfloat16 or wider, within the bound.
No kernel may reach another device: no remote copies, remote signals or barrier semaphores. Data moves between devices by JAX's collectives and lax.ppermute only.
A program may use at most 64 MiB of HBM per device.

v0:
```python
import functools

import jax
import jax.numpy as jnp
from jax import lax
from jax.experimental import pallas as pl
from jax.experimental.pallas import tpu as pltpu
from jax.sharding import PartitionSpec as P


WIDTH = 768
TERMS = 16
SECTORS = 16
PIECE = WIDTH // TERMS
QUARTER = WIDTH // 4
RINGS = TERMS // 2
JUMPS = (1, -1, 3)
BF16 = jnp.bfloat16
F32 = jnp.float32
VMEM = pl.BlockSpec(memory_space=pltpu.VMEM)
SMEM = pl.BlockSpec(memory_space=pltpu.SMEM)


def partner(stage, term, sector):
    ring, half = term // 2, term % 2
    if stage == 3:
        return 2 * ring + 1 - half
    sign = 1 - 2 * ((ring + sector) % 2)
    return 2 * ((ring + sign * JUMPS[stage] + RINGS) % RINGS) + half


def swap(block, where):
    route = []
    for term in range(TERMS):
        for sector in range(SECTORS):
            other_term, other_sector = where(term, sector)
            route.append((term * SECTORS + sector, other_term * SECTORS + other_sector))
    return lax.ppermute(block, ("term", "sec"), route)


def pair_sector(term, sector):
    return term, sector ^ 1


def next_sector(term, sector):
    return term, (sector + 1 if sector % 2 else sector - 1) % SECTORS


def stage_route(stage):
    return lambda term, sector: (partner(stage, term, sector), sector)


def far_route(term, sector):
    return partner(3, partner(2, term, sector), sector), sector


def sizes_here(sizes_ref, shift_ref):
    sector = lax.axis_index("sec")
    source = sector + shift_ref[0]
    inside = (source >= 0) & (source < SECTORS)
    source_size = jnp.where(inside, sizes_ref[jnp.clip(source, 0, SECTORS - 1)], 0)
    return sizes_ref[sector], source_size


def ones_below(size, start, count, dim):
    shape = (count, 1) if dim == 0 else (1, count)
    index = lax.broadcasted_iota(jnp.int32, shape, dim) + start
    return jnp.where(index < size, 1.0, 0.0).astype(BF16)


def piece_at(slot):
    term, sector = lax.axis_index("term"), lax.axis_index("sec")
    for stage in range(4):
        if not (slot >> (3 - stage)) & 1:
            term = partner(stage, term, sector)
    return term


def prepare_kernel(sizes_ref, shift_ref, left_ref, right_ref, site_ref, left_out, right_out, site_out):
    own, source = sizes_here(sizes_ref, shift_ref)
    own_columns = ones_below(own, 0, WIDTH, 1)
    source_columns = ones_below(source, 0, WIDTH, 1)
    for slot in range(TERMS):
        start = pl.multiple_of(piece_at(slot) * PIECE, 16)
        here = pl.ds(slot * PIECE, PIECE)
        rows = ones_below(own, start, PIECE, 0)
        left_out[here, :] = left_ref[pl.ds(start, PIECE), :] * rows * source_columns
        site_out[here, :] = site_ref[pl.ds(start, PIECE), :] * own_columns
        source_rows = ones_below(source, slot * PIECE, PIECE, 0)
        right_out[here, :] = right_ref[here, :] * source_rows * own_columns


def with_source(shift_ref, own_ref, pair_ref, next_ref, body):
    shift = shift_ref[0]
    even = lax.axis_index("sec") % 2 == 0
    local = shift == 0
    from_pair = (shift == 1) == even

    @pl.when(local)
    def _():
        body(own_ref)

    @pl.when(jnp.logical_not(local) & from_pair)
    def _():
        body(pair_ref)

    @pl.when(jnp.logical_not(local) & jnp.logical_not(from_pair))
    def _():
        body(next_ref)


def mix_kernel(shift_ref, own_ref, pair_ref, next_ref, right_ref, left_ref, mixed_out, send_out):
    def body(source_ref):
        mixed = jnp.dot(source_ref[...], right_ref[...], preferred_element_type=F32).astype(BF16)
        mixed_out[...] = mixed
        send_out[...] = jnp.dot(left_ref[:QUARTER, :], mixed, preferred_element_type=F32).astype(BF16)

    with_source(shift_ref, own_ref, pair_ref, next_ref, body)


def send_kernel(left_ref, mixed_ref, send_out):
    rows = left_ref[QUARTER : 2 * QUARTER, :]
    send_out[...] = jnp.dot(rows, mixed_ref[...], preferred_element_type=F32).astype(BF16)


def keep_kernel(left_ref, mixed_ref, after_ref, first_out, second_out):
    del after_ref
    for part, out in ((2, first_out), (3, second_out)):
        rows = left_ref[part * QUARTER : (part + 1) * QUARTER, :]
        out[...] = jnp.dot(rows, mixed_ref[...], preferred_element_type=F32)


def pass_kernel(keep_ref, got_ref, first_out, second_out):
    for here, out in ((pl.ds(0, PIECE), first_out), (pl.ds(PIECE, 3 * PIECE), second_out)):
        out[...] = (keep_ref[here, :] + got_ref[here, :].astype(F32)).astype(BF16)


def hold_kernel(keep_ref, got_ref, out_ref):
    out_ref[...] = keep_ref[...] + got_ref[...].astype(F32)


def split_kernel(start, hold_ref, got_ref, *outs):
    for slot, out in enumerate(outs):
        mine, theirs = pl.ds((start + slot) * PIECE, PIECE), pl.ds(slot * PIECE, PIECE)
        out[...] = (hold_ref[mine, :] + got_ref[theirs, :].astype(F32)).astype(out.dtype)


def finish_kernel(keep_ref, far_ref, ring_ref, half_ref, done_ref, out_ref):
    del done_ref
    total = keep_ref[...] + half_ref[...].astype(F32)
    out_ref[...] = total + (ring_ref[...].astype(F32) + far_ref[...].astype(F32))


def carry_kernel(shift_ref, own_ref, pair_ref, next_ref, left_ref, after_ref, out_ref):
    del after_ref

    def body(source_ref):
        carried = jnp.dot(left_ref[...], source_ref[...], preferred_element_type=F32)
        out_ref[...] = carried.astype(BF16)

    with_source(shift_ref, own_ref, pair_ref, next_ref, body)


def renew_kernel(sizes_ref, shift_ref, carried_ref, site_ref, after_ref, out_ref, done_ref):
    del after_ref
    done_ref[...] = jnp.zeros(done_ref.shape, F32)
    _, source_size = sizes_here(sizes_ref, shift_ref)
    carried = carried_ref[...] * ones_below(source_size, 0, WIDTH, 1)
    renewed = lax.dot_general(
        site_ref[...], carried, (((0,), (0,)), ((), ())), preferred_element_type=F32
    )
    out_ref[...] = renewed.astype(BF16)


def room(mebibytes):
    return pltpu.CompilerParams(vmem_limit_bytes=mebibytes * 1024 * 1024)


def cost(flops, moved):
    return pl.CostEstimate(flops=flops, bytes_accessed=moved, transcendentals=0)


def shards(state, left_environment, right_environment, site_blocks, sector_sizes, term_shift):
    square = jax.ShapeDtypeStruct((WIDTH, WIDTH), BF16)
    state_own, site_own = state[0], site_blocks[0]
    state_next = swap(state_own, next_sector)
    state_pair = swap(state_own, pair_sector)
    site_next = swap(site_own, next_sector)
    site_pair = swap(site_own, pair_sector)
    left, right, site = pl.pallas_call(
        prepare_kernel,
        out_shape=(square, square, square),
        in_specs=[SMEM, SMEM, VMEM, VMEM, VMEM],
        out_specs=(VMEM, VMEM, VMEM),
        cost_estimate=cost(6_000_000, 7_000_000),
        compiler_params=room(20),
        name="prepare",
    )(sector_sizes, term_shift, left_environment[0, 0], right_environment[0, 0], site_own)
    anywhere = pl.BlockSpec(memory_space=pl.ANY)
    strip = jax.ShapeDtypeStruct((QUARTER, WIDTH), BF16)
    strip_sum = jax.ShapeDtypeStruct((QUARTER, WIDTH), F32)
    strip_flops = 2 * QUARTER * WIDTH * WIDTH
    mixed, send_first = pl.pallas_call(
        mix_kernel,
        out_shape=(square, strip),
        in_specs=[SMEM] + [VMEM] * 5,
        out_specs=(VMEM, VMEM),
        compiler_params=room(20),
        cost_estimate=cost(5 * strip_flops, 6_000_000),
        name="mix",
    )(term_shift, state_own, state_pair, state_next, right, left)
    got_first = swap(send_first, stage_route(0))
    send_second = pl.pallas_call(
        send_kernel,
        out_shape=strip,
        in_specs=[VMEM, VMEM],
        out_specs=VMEM,
        compiler_params=room(12),
        cost_estimate=cost(strip_flops, 2_000_000),
        name="send",
    )(left, mixed)
    got_second = swap(send_second, stage_route(0))
    keep_first, keep_second = pl.pallas_call(
        keep_kernel,
        out_shape=(strip_sum, strip_sum),
        in_specs=[VMEM, VMEM, anywhere],
        out_specs=(VMEM, VMEM),
        compiler_params=room(12),
        cost_estimate=cost(2 * strip_flops, 3_000_000),
        name="keep",
    )(left, mixed, send_second)
    piece = jax.ShapeDtypeStruct((PIECE, WIDTH), BF16)
    pieces = jax.ShapeDtypeStruct((3 * PIECE, WIDTH), BF16)
    pass_first, pass_second = pl.pallas_call(
        pass_kernel,
        out_shape=(piece, pieces),
        in_specs=[VMEM, VMEM],
        out_specs=(VMEM, VMEM),
        compiler_params=room(6),
        cost_estimate=cost(QUARTER * WIDTH, 8 * QUARTER * WIDTH),
        name="pass",
    )(keep_first, got_first)
    moved_first = swap(pass_first, stage_route(1))
    moved_second = swap(pass_second, stage_route(1))
    held = pl.pallas_call(
        hold_kernel,
        out_shape=strip_sum,
        in_specs=[VMEM, VMEM],
        out_specs=VMEM,
        compiler_params=room(6),
        cost_estimate=cost(QUARTER * WIDTH, 8 * QUARTER * WIDTH),
        name="hold",
    )(keep_second, got_second)
    carried = pl.pallas_call(
        carry_kernel,
        out_shape=square,
        in_specs=[SMEM] + [VMEM] * 4 + [anywhere],
        out_specs=VMEM,
        compiler_params=room(12),
        cost_estimate=cost(4 * strip_flops, 5_000_000),
        name="carry",
    )(term_shift, site_own, site_pair, site_next, left, held)
    (far,) = pl.pallas_call(
        functools.partial(split_kernel, 0),
        out_shape=(piece,),
        in_specs=[VMEM, VMEM],
        out_specs=(VMEM,),
        compiler_params=room(6),
        cost_estimate=cost(PIECE * WIDTH, 8 * PIECE * WIDTH),
        name="split_first",
    )(held, moved_first)
    far_got = swap(far, far_route)
    ring, half, keep = pl.pallas_call(
        functools.partial(split_kernel, 1),
        out_shape=(piece, piece, jax.ShapeDtypeStruct((PIECE, WIDTH), F32)),
        in_specs=[VMEM, VMEM],
        out_specs=(VMEM, VMEM, VMEM),
        compiler_params=room(6),
        cost_estimate=cost(3 * PIECE * WIDTH, 24 * PIECE * WIDTH),
        name="split_second",
    )(held, moved_second)
    ring_got = swap(ring, stage_route(2))
    half_got = swap(half, stage_route(3))
    renewed, done = pl.pallas_call(
        renew_kernel,
        out_shape=(square, jax.ShapeDtypeStruct((8, 128), F32)),
        in_specs=[SMEM, SMEM, VMEM, VMEM, pl.BlockSpec(memory_space=pl.ANY)],
        out_specs=(VMEM, VMEM),
        compiler_params=room(12),
        cost_estimate=cost(2 * WIDTH * WIDTH * WIDTH, 4_000_000),
        name="renew",
    )(sector_sizes, term_shift, carried, site, keep)
    applied = pl.pallas_call(
        finish_kernel,
        out_shape=jax.ShapeDtypeStruct((PIECE, WIDTH), F32),
        in_specs=[VMEM] * 4 + [pl.BlockSpec(memory_space=pl.ANY)],
        out_specs=VMEM,
        compiler_params=room(4),
        cost_estimate=cost(4 * PIECE * WIDTH, 8 * PIECE * WIDTH),
        name="finish",
    )(keep, far_got, ring_got, half_got, done)
    return applied[None], renewed[None, None]


def solution(mesh):
    placed = (
        P("sec", None, None),
        P("term", "sec", None, None),
        P("term", "sec", None, None),
        P("sec", None, None),
        P(),
        P("term"),
    )
    return jax.shard_map(
        shards,
        mesh=mesh,
        in_specs=placed,
        out_specs=(P("sec", "term", None), P("term", "sec", None, None)),
        check_vma=False,
    )
```

profile of v0, /device:TPU:1, one launch (start us, length us, event | category | flops | bytes accessed | tf_op | source)
XLA Modules:
  0.0 51.7 jit_solution(10248641584028358993)
XLA Ops:
  0.6 3.3 %collective-permute-start = (bf16[768,768]{1,0:T(8,128)(2,1)}, bf16[768,768]{1,0:T(8,128)(2,1)S(1)}, u32[]{:S(2)}, u32[]{:S(2)}) collective-permute-start(bf16[768,768]{1,0:T(8,128)(2,1)} %bitcast.12), channel_id=1, source_target_pairs={{0,1},{1,0},{2,3},{3,2},{4,5},{5,4},{6,7},{7,6},{8,9},{9,8},{10,11... | collective-permute-start | bytes 3538952 | tf_op jit(solution)/shard_map/ppermute | solution.py:38
  3.9 0.0 collective-permute-start.1
  3.9 2.2 %collective-permute-start.9 = (bf16[768,768]{1,0:T(8,128)(2,1)}, bf16[768,768]{1,0:T(8,128)(2,1)S(1)}, u32[]{:S(2)}, u32[]{:S(2)}) collective-permute-start(bf16[768,768]{1,0:T(8,128)(2,1)} %bitcast.6), channel_id=1, source_target_pairs={{0,1},{1,0},{2,3},{3,2},{4,5},{5,4},{6,7},{7,6},{8,9},{9,8},{10,11... | collective-permute-start | bytes 3538952 | tf_op jit(solution)/shard_map/ppermute | solution.py:38
  6.1 0.0 collective-permute-start.10
  6.8 0.0 copy-start
  6.8 1.3 %copy-done = bf16[1,768,768]{2,1,0:T(8,128)(2,1)S(1)} copy-done((bf16[1,768,768]{2,1,0:T(8,128)(2,1)S(1)}, bf16[1,768,768]{2,1,0:T(8,128)(2,1)}, u32[]{:S(2)}) %copy-start) | copy-done | bytes 1179672
  8.0 0.0 copy-start.2
  8.0 1.3 %copy-done.2 = bf16[1,1,768,768]{3,2,1,0:T(8,128)(2,1)S(1)} copy-done((bf16[1,1,768,768]{3,2,1,0:T(8,128)(2,1)S(1)}, bf16[1,1,768,768]{3,2,1,0:T(8,128)(2,1)}, u32[]{:S(2)}) %copy-start.2) | copy-done | bytes 1179672
  9.3 0.0 copy-start.3
  9.3 1.3 %copy-done.3 = bf16[1,1,768,768]{3,2,1,0:T(8,128)(2,1)S(1)} copy-done((bf16[1,1,768,768]{3,2,1,0:T(8,128)(2,1)S(1)}, bf16[1,1,768,768]{3,2,1,0:T(8,128)(2,1)}, u32[]{:S(2)}) %copy-start.3) | copy-done | bytes 1179672
  10.6 0.0 copy-start.5
  10.6 0.7 %copy-done.5 = s32[16]{0:T(128)S(1)} copy-done((s32[16]{0:T(128)S(1)}, s32[16]{0:T(128)}, u32[]{:S(2)}) %copy-start.5) | copy-done | bytes 88
  11.2 0.0 copy-start.4
  11.2 0.9 %prepare.1 = (bf16[768,768]{1,0:T(8,128)(2,1)S(1)}, bf16[768,768]{1,0:T(8,128)(2,1)S(1)}, bf16[768,768]{1,0:T(8,128)(2,1)S(1)}) custom-call(s32[16]{0:T(128)S(1)} %copy-done.5, s32[1]{0:T(128)S(6)} %copy.8.shift_ref, bf16[768,768]{1,0:T(8,128)(2,1)S(1)} %bitcast.10, bf16[768,768]{1,0:T(8,128)(2,1)S(1)} %bitcast.11, bf16[768,768]{1,0:T(8,128)(2,1)S(1)} %bitcast.8), custom_call_target="tpu_custom_call" | custom-call | flops 6000000 | bytes 7000000 | tf_op jit(solution)/shard_map/prepare/pallas_call | solution.py:190
  12.1 0.0 collective-permute-done.pair_ref
  12.1 7.9 %collective-permute-done.1.next_ref = bf16[768,768]{1,0:T(8,128)(2,1)S(1)} collective-permute-done((bf16[768,768]{1,0:T(8,128)(2,1)}, bf16[768,768]{1,0:T(8,128)(2,1)S(1)}, u32[]{:S(2)}, u32[]{:S(2)}) %collective-permute-start.1) | collective-permute-done | bytes 1179680 | tf_op jit(solution)/shard_map/ppermute | solution.py:38
  20.1 0.0 copy-done.4
  20.1 1.5 %mix.1 = (bf16[768,768]{1,0:T(8,128)(2,1)S(1)}, bf16[192,768]{1,0:T(8,128)(2,1)S(1)}) custom-call(s32[1]{0:T(128)S(6)} %copy.8.shift_ref, bf16[768,768]{1,0:T(8,128)(2,1)S(1)} %bitcast.14, bf16[768,768]{1,0:T(8,128)(2,1)S(1)} %collective-permute-done.pair_ref, bf16[768,768]{1,0:T(8,128)(2,1)S(1)} %collective-permute-done.1.next_ref, ...), custom_call_target="tpu_custom_call" | custom-call | flops 1132462080 | bytes 6000000 | tf_op jit(solution)/shard_map/mix/pallas_call | solution.py:203
  21.6 4.0 %collective-permute-start.3 = (bf16[192,768]{1,0:T(8,128)(2,1)S(1)}, bf16[192,768]{1,0:T(8,128)(2,1)S(1)}, u32[]{:S(2)}, u32[]{:S(2)}) collective-permute-start(bf16[192,768]{1,0:T(8,128)(2,1)S(1)} %get-tuple-element.21), channel_id=1, source_target_pairs={{0,32},{1,225},{2,34},{3,227},{4,36},{5,229},{6,38},{7,231},{8,40}... | collective-permute-start | bytes 884744 | tf_op jit(solution)/shard_map/ppermute | solution.py:38
  25.5 0.4 send.1.after_ref
  25.9 0.1 collective-permute-start.2
  26.0 0.6 %keep.1 = (f32[192,768]{1,0:T(8,128)S(1)}, f32[192,768]{1,0:T(8,128)S(1)}) custom-call(bf16[768,768]{1,0:T(8,128)(2,1)S(1)} %get-tuple-element.16.left_ref, bf16[768,768]{1,0:T(8,128)(2,1)S(1)} %get-tuple-element.18.mixed_ref, bf16[192,768]{1,0:T(8,128)(2,1)S(1)} %send.1.after_ref), custom_call_target="tpu_custom_call" | custom-call | flops 452984832 | bytes 3000000 | tf_op jit(solution)/shard_map/keep/pallas_call | solution.py:223
  26.7 3.3 %collective-permute-done.3.got_ref = bf16[192,768]{1,0:T(8,128)(2,1)S(1)} collective-permute-done((bf16[192,768]{1,0:T(8,128)(2,1)S(1)}, bf16[192,768]{1,0:T(8,128)(2,1)S(1)}, u32[]{:S(2)}, u32[]{:S(2)}) %collective-permute-start.3) | collective-permute-done | bytes 294944 | tf_op jit(solution)/shard_map/ppermute | solution.py:38
  29.9 0.0 copy-start.1
  29.9 0.1 pass.1
  30.0 0.1 collective-permute-start.4
  30.1 1.5 %collective-permute-start.5 = (bf16[48,768]{1,0:T(8,128)(2,1)S(1)}, bf16[48,768]{1,0:T(8,128)(2,1)S(1)}, u32[]{:S(2)}, u32[]{:S(2)}) collective-permute-start(bf16[48,768]{1,0:T(8,128)(2,1)S(1)} %get-tuple-element.24), channel_id=1, source_target_pairs={{0,224},{1,33},{2,226},{3,35},{4,228},{5,37},{6,230},{7,39},{8,232... | collective-permute-start | bytes 221192 | tf_op jit(solution)/shard_map/ppermute | solution.py:38
  31.5 1.6 %collective-permute-done.2.got_ref = bf16[192,768]{1,0:T(8,128)(2,1)S(1)} collective-permute-done((bf16[192,768]{1,0:T(8,128)(2,1)S(1)}, bf16[192,768]{1,0:T(8,128)(2,1)S(1)}, u32[]{:S(2)}, u32[]{:S(2)}) %collective-permute-start.2) | collective-permute-done | bytes 294944 | tf_op jit(solution)/shard_map/ppermute | solution.py:38
  33.1 0.1 hold.1.hold_ref.after_ref
  33.1 0.0 collective-permute-done.9.pair_ref
  33.1 0.0 collective-permute-done.10.next_ref
  33.2 0.0 copy-done.1
  33.2 1.1 %carry.1.carried_ref = bf16[768,768]{1,0:T(8,128)(2,1)S(1)} custom-call(s32[1]{0:T(128)S(6)} %copy.8.shift_ref, bf16[768,768]{1,0:T(8,128)(2,1)S(1)} %bitcast.9, bf16[768,768]{1,0:T(8,128)(2,1)S(1)} %collective-permute-done.9.pair_ref, bf16[768,768]{1,0:T(8,128)(2,1)S(1)} %collective-permute-done.10.next_ref, ...), custom_call_target="tpu_custom_call" | custom-call | flops 905969664 | bytes 5000000 | tf_op jit(solution)/shard_map/carry/pallas_call | solution.py:254
  34.3 0.0 copy-start.6
  34.3 1.9 %collective-permute-done.5.got_ref = bf16[48,768]{1,0:T(8,128)(2,1)S(1)} collective-permute-done((bf16[48,768]{1,0:T(8,128)(2,1)S(1)}, bf16[48,768]{1,0:T(8,128)(2,1)S(1)}, u32[]{:S(2)}, u32[]{:S(2)}) %collective-permute-start.5) | collective-permute-done | bytes 73760 | tf_op jit(solution)/shard_map/ppermute | solution.py:38
  36.2 7.5 %collective-permute-start.6 = (bf16[48,768]{1,0:T(8,128)(2,1)S(1)}, bf16[48,768]{1,0:T(8,128)(2,1)S(1)}, u32[]{:S(2)}, u32[]{:S(2)}) collective-permute-start(bf16[48,768]{1,0:T(8,128)(2,1)S(1)} %split_first.1), channel_id=1, source_target_pairs={{0,112},{1,177},{2,114},{3,179},{4,116},{5,181},{6,118},{7,183},{8... | collective-permute-start | bytes 221192 | tf_op jit(solution)/shard_map/ppermute | solution.py:38
  43.7 0.0 collective-permute-done.4.got_ref
  43.7 0.1 collective-permute-start.7
  43.8 0.3 collective-permute-start.8
  44.1 0.0 copy-done.6
  44.1 2.7 %renew.1 = (bf16[768,768]{1,0:T(8,128)(2,1)}, f32[8,128]{1,0:T(8,128)S(1)}) custom-call(s32[16]{0:T(128)S(1)} %copy-done.6, s32[1]{0:T(128)S(6)} %copy.8.shift_ref, bf16[768,768]{1,0:T(8,128)(2,1)S(1)} %carry.1.carried_ref, bf16[768,768]{1,0:T(8,128)(2,1)S(1)} %get-tuple-element.27.site_ref, f32[48,768]{1,0:T(8,128)S(1)} %get-tuple-element.23.after_ref.keep_ref), custom_call_target="tpu_custom_call" | custom-call | flops 905969664 | bytes 4000000 | tf_op jit(solution)/shard_map/renew/pallas_call | solution.py:284
  46.8 0.0 collective-permute-done.6.far_ref
  46.8 4.2 %collective-permute-done.7.ring_ref = bf16[48,768]{1,0:T(8,128)(2,1)S(1)} collective-permute-done((bf16[48,768]{1,0:T(8,128)(2,1)S(1)}, bf16[48,768]{1,0:T(8,128)(2,1)S(1)}, u32[]{:S(2)}, u32[]{:S(2)}) %collective-permute-start.7) | collective-permute-done | bytes 73760 | tf_op jit(solution)/shard_map/ppermute | solution.py:38
  51.0 0.0 collective-permute-done.8.half_ref
  51.0 0.7 %finish.1 = f32[48,768]{1,0:T(8,128)} custom-call(f32[48,768]{1,0:T(8,128)S(1)} %get-tuple-element.23.after_ref.keep_ref, bf16[48,768]{1,0:T(8,128)(2,1)S(1)} %collective-permute-done.6.far_ref, bf16[48,768]{1,0:T(8,128)(2,1)S(1)} %collective-permute-done.7.ring_ref, bf16[48,768]{1,0:T(8,128)(2,1)S(1)} %collective-permute-done.8.half_ref, ...), custom_call_target="tpu_custom_call" | custom-call | flops 147456 | bytes 294912 | tf_op jit(solution)/shard_map/finish/pallas_call | solution.py:293
  (2 shorter events, 0.1 us)
Async XLA Ops:
  0.6 11.5 %collective-permute-start = (bf16[768,768]{1,0:T(8,128)(2,1)}, bf16[768,768]{1,0:T(8,128)(2,1)S(1)}, u32[]{:S(2)}, u32[]{:S(2)}) collective-permute-start(bf16[768,768]{1,0:T(8,128)(2,1)} %bitcast.12), channel_id=1, source_target_pairs={{0,1},{1,0},{2,3},{3,2},{4,5},{5,4},{6,7},{7,6},{8,9},{9,8},{10,11... | collective-permute-start | bytes 3538952 | tf_op jit(solution)/shard_map/ppermute | solution.py:38
  3.9 16.1 %collective-permute-start.1 = (bf16[768,768]{1,0:T(8,128)(2,1)}, bf16[768,768]{1,0:T(8,128)(2,1)S(1)}, u32[]{:S(2)}, u32[]{:S(2)}) collective-permute-start(bf16[768,768]{1,0:T(8,128)(2,1)} %bitcast.13), channel_id=1, source_target_pairs={{0,15},{1,2},{2,1},{3,4},{4,3},{5,6},{6,5},{7,8},{8,7},{9,10},{10,... | collective-permute-start | bytes 3538952 | tf_op jit(solution)/shard_map/ppermute | solution.py:38
  3.9 29.2 %collective-permute-start.9 = (bf16[768,768]{1,0:T(8,128)(2,1)}, bf16[768,768]{1,0:T(8,128)(2,1)S(1)}, u32[]{:S(2)}, u32[]{:S(2)}) collective-permute-start(bf16[768,768]{1,0:T(8,128)(2,1)} %bitcast.6), channel_id=1, source_target_pairs={{0,1},{1,0},{2,3},{3,2},{4,5},{5,4},{6,7},{7,6},{8,9},{9,8},{10,11... | collective-permute-start | bytes 3538952 | tf_op jit(solution)/shard_map/ppermute | solution.py:38
  6.1 27.1 %collective-permute-start.10 = (bf16[768,768]{1,0:T(8,128)(2,1)}, bf16[768,768]{1,0:T(8,128)(2,1)S(1)}, u32[]{:S(2)}, u32[]{:S(2)}) collective-permute-start(bf16[768,768]{1,0:T(8,128)(2,1)} %bitcast.7), channel_id=1, source_target_pairs={{0,15},{1,2},{2,1},{3,4},{4,3},{5,6},{6,5},{7,8},{8,7},{9,10},{10,... | collective-permute-start | bytes 3538952 | tf_op jit(solution)/shard_map/ppermute | solution.py:38
  6.8 1.3 %copy-start = (bf16[1,768,768]{2,1,0:T(8,128)(2,1)S(1)}, bf16[1,768,768]{2,1,0:T(8,128)(2,1)}, u32[]{:S(2)}) copy-start(bf16[1,768,768]{2,1,0:T(8,128)(2,1)} %param.9) | copy-start | bytes 3538948
  8.0 1.3 %copy-start.2 = (bf16[1,1,768,768]{3,2,1,0:T(8,128)(2,1)S(1)}, bf16[1,1,768,768]{3,2,1,0:T(8,128)(2,1)}, u32[]{:S(2)}) copy-start(bf16[1,1,768,768]{3,2,1,0:T(8,128)(2,1)} %param.7) | copy-start | bytes 3538948
  9.3 1.3 %copy-start.3 = (bf16[1,1,768,768]{3,2,1,0:T(8,128)(2,1)S(1)}, bf16[1,1,768,768]{3,2,1,0:T(8,128)(2,1)}, u32[]{:S(2)}) copy-start(bf16[1,1,768,768]{3,2,1,0:T(8,128)(2,1)} %param.8) | copy-start | bytes 3538948
  10.6 0.7 %copy-start.5 = (s32[16]{0:T(128)S(1)}, s32[16]{0:T(128)}, u32[]{:S(2)}) copy-start(s32[16]{0:T(128)} %sizes_ref.3) | copy-start | bytes 196
  11.2 8.8 %copy-start.4 = (bf16[1,768,768]{2,1,0:T(8,128)(2,1)S(1)}, bf16[1,768,768]{2,1,0:T(8,128)(2,1)}, u32[]{:S(2)}) copy-start(bf16[1,768,768]{2,1,0:T(8,128)(2,1)} %param.6) | copy-start | bytes 3538948
  21.6 8.4 %collective-permute-start.3 = (bf16[192,768]{1,0:T(8,128)(2,1)S(1)}, bf16[192,768]{1,0:T(8,128)(2,1)S(1)}, u32[]{:S(2)}, u32[]{:S(2)}) collective-permute-start(bf16[192,768]{1,0:T(8,128)(2,1)S(1)} %get-tuple-element.21), channel_id=1, source_target_pairs={{0,32},{1,225},{2,34},{3,227},{4,36},{5,229},{6,38},{7,231},{8,40}... | collective-permute-start | bytes 884744 | tf_op jit(solution)/shard_map/ppermute | solution.py:38
  25.9 7.2 %collective-permute-start.2 = (bf16[192,768]{1,0:T(8,128)(2,1)S(1)}, bf16[192,768]{1,0:T(8,128)(2,1)S(1)}, u32[]{:S(2)}, u32[]{:S(2)}) collective-permute-start(bf16[192,768]{1,0:T(8,128)(2,1)S(1)} %send.1.after_ref), channel_id=1, source_target_pairs={{0,32},{1,225},{2,34},{3,227},{4,36},{5,229},{6,38},{7,231},{8,40}... | collective-permute-start | bytes 884744 | tf_op jit(solution)/shard_map/ppermute | solution.py:38
  29.9 3.2 %copy-start.1 = (bf16[1,768,768]{2,1,0:T(8,128)(2,1)S(1)}, bf16[1,768,768]{2,1,0:T(8,128)(2,1)}, u32[]{:S(2)}) copy-start(bf16[1,768,768]{2,1,0:T(8,128)(2,1)} %param.9) | copy-start | bytes 3538948
  30.0 13.7 %collective-permute-start.4 = (bf16[144,768]{1,0:T(8,128)(2,1)S(1)}, bf16[144,768]{1,0:T(8,128)(2,1)S(1)}, u32[]{:S(2)}, u32[]{:S(2)}) collective-permute-start(bf16[144,768]{1,0:T(8,128)(2,1)S(1)} %get-tuple-element.22), channel_id=1, source_target_pairs={{0,224},{1,33},{2,226},{3,35},{4,228},{5,37},{6,230},{7,39},{8,232... | collective-permute-start | bytes 663560 | tf_op jit(solution)/shard_map/ppermute | solution.py:38
  30.1 6.1 %collective-permute-start.5 = (bf16[48,768]{1,0:T(8,128)(2,1)S(1)}, bf16[48,768]{1,0:T(8,128)(2,1)S(1)}, u32[]{:S(2)}, u32[]{:S(2)}) collective-permute-start(bf16[48,768]{1,0:T(8,128)(2,1)S(1)} %get-tuple-element.24), channel_id=1, source_target_pairs={{0,224},{1,33},{2,226},{3,35},{4,228},{5,37},{6,230},{7,39},{8,232... | collective-permute-start | bytes 221192 | tf_op jit(solution)/shard_map/ppermute | solution.py:38
  34.3 9.9 %copy-start.6 = (s32[16]{0:T(128)S(1)}, s32[16]{0:T(128)}, u32[]{:S(2)}) copy-start(s32[16]{0:T(128)} %sizes_ref.3) | copy-start | bytes 196
  36.2 10.6 %collective-permute-start.6 = (bf16[48,768]{1,0:T(8,128)(2,1)S(1)}, bf16[48,768]{1,0:T(8,128)(2,1)S(1)}, u32[]{:S(2)}, u32[]{:S(2)}) collective-permute-start(bf16[48,768]{1,0:T(8,128)(2,1)S(1)} %split_first.1), channel_id=1, source_target_pairs={{0,112},{1,177},{2,114},{3,179},{4,116},{5,181},{6,118},{7,183},{8... | collective-permute-start | bytes 221192 | tf_op jit(solution)/shard_map/ppermute | solution.py:38
  43.7 7.3 %collective-permute-start.7 = (bf16[48,768]{1,0:T(8,128)(2,1)S(1)}, bf16[48,768]{1,0:T(8,128)(2,1)S(1)}, u32[]{:S(2)}, u32[]{:S(2)}) collective-permute-start(bf16[48,768]{1,0:T(8,128)(2,1)S(1)} %get-tuple-element.25), channel_id=1, source_target_pairs={{0,96},{1,161},{2,98},{3,163},{4,100},{5,165},{6,102},{7,167},{8,1... | collective-permute-start | bytes 221192 | tf_op jit(solution)/shard_map/ppermute | solution.py:38
  43.8 7.2 %collective-permute-start.8 = (bf16[48,768]{1,0:T(8,128)(2,1)S(1)}, bf16[48,768]{1,0:T(8,128)(2,1)S(1)}, u32[]{:S(2)}, u32[]{:S(2)}) collective-permute-start(bf16[48,768]{1,0:T(8,128)(2,1)S(1)} %get-tuple-element.26), channel_id=1, source_target_pairs={{0,16},{1,17},{2,18},{3,19},{4,20},{5,21},{6,22},{7,23},{8,24},{9,... | collective-permute-start | bytes 221192 | tf_op jit(solution)/shard_map/ppermute | solution.py:38
where the time goes:
time: 51.9 us; the launch traced here: 51.7 us
  starting transfers between devices  18.9 us (36%)
  waiting for transfers between devices  18.8 us (36%)
  Pallas kernels  8.07 us (16%)
  local copies, waits for them, and re-layouts  4.47 us (9%)
  between operations  1.41 us (3%)
    ppermute x11, starting transfers between devices, swap(): return lax.ppermute(block, ('term', 'sec'), route)  18.9 us
    ppermute x11, waiting for transfers between devices, swap(): return lax.ppermute(block, ('term', 'sec'), route)  18.8 us
    unnamed x14, local copies, waits for them, and re-layouts  4.47 us
    pallas_call x1, Pallas kernels, shards(): pl.pallas_call(renew_kernel, out_shape=(square, jax.ShapeDtypeStruct((8,...  2.69 us
    pallas_call x1, Pallas kernels, shards(): pl.pallas_call(mix_kernel, out_shape=(square, strip), in_specs=[SMEM] + [...  1.49 us
    pallas_call x1, Pallas kernels, shards(): pl.pallas_call(carry_kernel, out_shape=square, in_specs=[SMEM] + [VMEM] *...  1.11 us
  transfers between devices with their start and end apart: 11, of which 5 were waited for; matrix products, arithmetic and copies ran while one was open for 0% of the time, Pallas kernels for 13%

commit v1 on v0

--- a/solution.py
+++ b/solution.py
@@ -13,12 +13,15 @@
 SECTORS = 16
 PIECE = WIDTH // TERMS
 QUARTER = WIDTH // 4
+RELAYED = 160
+DIRECT = WIDTH - 2 * RELAYED
 RINGS = TERMS // 2
 JUMPS = (1, -1, 3)
 BF16 = jnp.bfloat16
 F32 = jnp.float32
 VMEM = pl.BlockSpec(memory_space=pltpu.VMEM)
 SMEM = pl.BlockSpec(memory_space=pltpu.SMEM)
+HBM = pl.BlockSpec(memory_space=pltpu.HBM)
 
 
 def partner(stage, term, sector):
@@ -76,10 +79,56 @@
     return term
 
 
-def prepare_kernel(sizes_ref, shift_ref, left_ref, right_ref, site_ref, left_out, right_out, site_out):
+def relay_starts():
+    odd = (lax.axis_index("term") // 2 + lax.axis_index("sec")) % 2
+    taken = DIRECT + RELAYED * odd
+    passed = DIRECT + RELAYED * (1 - odd)
+    return pl.multiple_of(taken, 16), pl.multiple_of(passed, 16)
+
+
+def cut_kernel(state_ref, shared_out, direct_out, sems):
+    others = relay_starts()[1]
+    shared = pltpu.make_async_copy(state_ref.at[pl.ds(others, RELAYED), :], shared_out, sems.at[0])
+    direct = pltpu.make_async_copy(state_ref.at[pl.ds(0, DIRECT), :], direct_out, sems.at[1])
+    shared.start()
+    direct.start()
+    shared.wait()
+    direct.wait()
+
+
+def bring_kernel(state_ref, site_ref, out_ref, turned_out, sem):
+    copy = pltpu.make_async_copy(state_ref, out_ref, sem)
+    copy.start()
+    turned_out[...] = site_ref[...].T
+    copy.wait()
+
+
+def prepare_kernel(
+    sizes_ref,
+    shift_ref,
+    left_hbm,
+    right_hbm,
+    site_hbm,
+    left_out,
+    right_out,
+    site_out,
+    left_ref,
+    right_ref,
+    site_ref,
+    sems,
+):
+    moves = ((left_hbm, left_ref), (right_hbm, right_ref), (site_hbm, site_ref))
+    copies = [
+        pltpu.make_async_copy(source, target, sems.at[index])
+        for index, (source, target) in enumerate(moves)
+    ]
+    for copy in copies:
+        copy.start()
     own, source = sizes_here(sizes_ref, shift_ref)
     own_columns = ones_below(own, 0, WIDTH, 1)
     source_columns = ones_below(source, 0, WIDTH, 1)
+    for copy in copies:
+        copy.wait()
     for slot in range(TERMS):
         start = pl.multiple_of(piece_at(slot) * PIECE, 16)
         here = pl.ds(slot * PIECE, PIECE)
@@ -90,32 +139,43 @@
         right_out[here, :] = right_ref[here, :] * source_rows * own_columns
 
 
-def with_source(shift_ref, own_ref, pair_ref, next_ref, body):
+def with_source(shift_ref, own, pair, far):
     shift = shift_ref[0]
     even = lax.axis_index("sec") % 2 == 0
     local = shift == 0
     from_pair = (shift == 1) == even
 
-    @pl.when(local)
-    def _():
-        body(own_ref)
-
-    @pl.when(jnp.logical_not(local) & from_pair)
-    def _():
-        body(pair_ref)
-
-    @pl.when(jnp.logical_not(local) & jnp.logical_not(from_pair))
-    def _():
-        body(next_ref)
-
-
-def mix_kernel(shift_ref, own_ref, pair_ref, next_ref, right_ref, left_ref, mixed_out, send_out):
+    pl.when(local)(own)
+    pl.when(jnp.logical_not(local) & from_pair)(pair)
+    pl.when(jnp.logical_not(local) & jnp.logical_not(from_pair))(far)
+
+
+def mix_kernel(
+    shift_ref,
+    own_ref,
+    pair_ref,
+    direct_ref,
+    taken_ref,
+    passed_ref,
+    right_ref,
+    left_ref,
+    mixed_out,
+    send_out,
+    joined_ref,
+):
     def body(source_ref):
         mixed = jnp.dot(source_ref[...], right_ref[...], preferred_element_type=F32).astype(BF16)
         mixed_out[...] = mixed
         send_out[...] = jnp.dot(left_ref[:QUARTER, :], mixed, preferred_element_type=F32).astype(BF16)
 
-    with_source(shift_ref, own_ref, pair_ref, next_ref, body)
+    def joined():
+        taken, passed = relay_starts()
+        joined_ref[:DIRECT, :] = direct_ref[...]
+        joined_ref[pl.ds(taken, RELAYED), :] = taken_ref[...]
+        joined_ref[pl.ds(passed, RELAYED), :] = passed_ref[...]
+        body(joined_ref)
+
+    with_source(shift_ref, lambda: body(own_ref), lambda: body(pair_ref), joined)
 
 
 def send_kernel(left_ref, mixed_ref, send_out):
@@ -151,25 +211,36 @@
     out_ref[...] = total + (ring_ref[...].astype(F32) + far_ref[...].astype(F32))
 
 
-def carry_kernel(shift_ref, own_ref, pair_ref, next_ref, left_ref, after_ref, out_ref):
+def carry_kernel(part, shift_ref, own_ref, pair_ref, next_ref, left_ref, after_ref, out_ref):
     del after_ref
+    rows = pl.ds(part * 2 * QUARTER, 2 * QUARTER)
 
     def body(source_ref):
-        carried = jnp.dot(left_ref[...], source_ref[...], preferred_element_type=F32)
+        carried = jnp.dot(left_ref[rows, :], source_ref[...], preferred_element_type=F32)
         out_ref[...] = carried.astype(BF16)
 
-    with_source(shift_ref, own_ref, pair_ref, next_ref, body)
-
-
-def renew_kernel(sizes_ref, shift_ref, carried_ref, site_ref, after_ref, out_ref, done_ref):
+    with_source(shift_ref, *(functools.partial(body, ref) for ref in (own_ref, pair_ref, next_ref)))
+
+
+def renew_kernel(
+    sizes_ref, shift_ref, upper_ref, lower_ref, site_ref, after_ref, out_hbm, done_ref, rows_ref, sems
+):
     del after_ref
     done_ref[...] = jnp.zeros(done_ref.shape, F32)
     _, source_size = sizes_here(sizes_ref, shift_ref)
-    carried = carried_ref[...] * ones_below(source_size, 0, WIDTH, 1)
-    renewed = lax.dot_general(
-        site_ref[...], carried, (((0,), (0,)), ((), ())), preferred_element_type=F32
-    )
-    out_ref[...] = renewed.astype(BF16)
+    columns = ones_below(source_size, 0, WIDTH, 1)
+    carried = jnp.concatenate([upper_ref[...] * columns, lower_ref[...] * columns], axis=0)
+    copies = []
+    for part in range(4):
+        here = pl.ds(part * QUARTER, QUARTER)
+        renewed = jnp.dot(site_ref[here, :], carried, preferred_element_type=F32)
+        rows_ref[here, :] = renewed.astype(BF16)
+        copies.append(
+            pltpu.make_async_copy(rows_ref.at[here, :], out_hbm.at[here, :], sems.at[part])
+        )
+        copies[-1].start()
+    for copy in copies:
+        copy.wait()
 
 
 def room(mebibytes):
@@ -183,19 +254,45 @@
 def shards(state, left_environment, right_environment, site_blocks, sector_sizes, term_shift):
     square = jax.ShapeDtypeStruct((WIDTH, WIDTH), BF16)
     state_own, site_own = state[0], site_blocks[0]
-    state_next = swap(state_own, next_sector)
+    shared, direct = pl.pallas_call(
+        cut_kernel,
+        out_shape=(
+            jax.ShapeDtypeStruct((RELAYED, WIDTH), BF16),
+            jax.ShapeDtypeStruct((DIRECT, WIDTH), BF16),
+        ),
+        in_specs=[HBM],
+        out_specs=(VMEM, VMEM),
+        scratch_shapes=[pltpu.SemaphoreType.DMA((2,))],
+        compiler_params=room(4),
+        cost_estimate=cost(1000, 2_000_000),
+        name="cut",
+    )(state_own)
+    taken = swap(shared, next_sector)
+    direct_got = swap(direct, next_sector)
     state_pair = swap(state_own, pair_sector)
+    passed = swap(taken, stage_route(0))
     site_next = swap(site_own, next_sector)
     site_pair = swap(site_own, pair_sector)
     left, right, site = pl.pallas_call(
         prepare_kernel,
-        out_shape=(square, square, square),
-        in_specs=[SMEM, SMEM, VMEM, VMEM, VMEM],
-        out_specs=(VMEM, VMEM, VMEM),
-        cost_estimate=cost(6_000_000, 7_000_000),
-        compiler_params=room(20),
+        out_shape=(square,) * 3,
+        in_specs=[SMEM, SMEM] + [HBM] * 3,
+        out_specs=(VMEM,) * 3,
+        scratch_shapes=[pltpu.VMEM((WIDTH, WIDTH), BF16)] * 3 + [pltpu.SemaphoreType.DMA((3,))],
+        compiler_params=room(12),
+        cost_estimate=cost(6_000_000, 1000),
         name="prepare",
     )(sector_sizes, term_shift, left_environment[0, 0], right_environment[0, 0], site_own)
+    state_here, turned = pl.pallas_call(
+        bring_kernel,
+        out_shape=(square, square),
+        in_specs=[HBM, VMEM],
+        out_specs=(VMEM, VMEM),
+        scratch_shapes=[pltpu.SemaphoreType.DMA],
+        compiler_params=room(10),
+        cost_estimate=cost(1000, 2_400_000),
+        name="bring",
+    )(state_own, site)
     anywhere = pl.BlockSpec(memory_space=pl.ANY)
     strip = jax.ShapeDtypeStruct((QUARTER, WIDTH), BF16)
     strip_sum = jax.ShapeDtypeStruct((QUARTER, WIDTH), F32)
@@ -203,12 +300,13 @@
     mixed, send_first = pl.pallas_call(
         mix_kernel,
         out_shape=(square, strip),
-        in_specs=[SMEM] + [VMEM] * 5,
+        in_specs=[SMEM] + [VMEM] * 7,
         out_specs=(VMEM, VMEM),
+        scratch_shapes=[pltpu.VMEM((WIDTH, WIDTH), BF16)],
         compiler_params=room(20),
         cost_estimate=cost(5 * strip_flops, 6_000_000),
         name="mix",
-    )(term_shift, state_own, state_pair, state_next, right, left)
+    )(term_shift, state_here, state_pair, direct_got, taken, passed, right, left)
     got_first = swap(send_first, stage_route(0))
     send_second = pl.pallas_call(
         send_kernel,
@@ -251,15 +349,19 @@
         cost_estimate=cost(QUARTER * WIDTH, 8 * QUARTER * WIDTH),
         name="hold",
     )(keep_second, got_second)
-    carried = pl.pallas_call(
-        carry_kernel,
-        out_shape=square,
-        in_specs=[SMEM] + [VMEM] * 4 + [anywhere],
-        out_specs=VMEM,
-        compiler_params=room(12),
-        cost_estimate=cost(4 * strip_flops, 5_000_000),
-        name="carry",
-    )(term_shift, site_own, site_pair, site_next, left, held)
+
+    def carry(part, after):
+        return pl.pallas_call(
+            functools.partial(carry_kernel, part),
+            out_shape=jax.ShapeDtypeStruct((2 * QUARTER, WIDTH), BF16),
+            in_specs=[SMEM] + [VMEM] * 4 + [anywhere],
+            out_specs=VMEM,
+            compiler_params=room(12),
+            cost_estimate=cost(2 * strip_flops, 4_000_000),
+            name="carry",
+        )(term_shift, site_own, site_pair, site_next, left, after)
+
+    upper = carry(0, held)
     (far,) = pl.pallas_call(
         functools.partial(split_kernel, 0),
         out_shape=(piece,),
@@ -281,15 +383,17 @@
     )(held, moved_second)
     ring_got = swap(ring, stage_route(2))
     half_got = swap(half, stage_route(3))
+    lower = carry(1, keep)
     renewed, done = pl.pallas_call(
         renew_kernel,
         out_shape=(square, jax.ShapeDtypeStruct((8, 128), F32)),
-        in_specs=[SMEM, SMEM, VMEM, VMEM, pl.BlockSpec(memory_space=pl.ANY)],
-        out_specs=(VMEM, VMEM),
+        in_specs=[SMEM, SMEM] + [VMEM] * 3 + [anywhere],
+        out_specs=(HBM, VMEM),
+        scratch_shapes=[pltpu.VMEM((WIDTH, WIDTH), BF16), pltpu.SemaphoreType.DMA((4,))],
         compiler_params=room(12),
         cost_estimate=cost(2 * WIDTH * WIDTH * WIDTH, 4_000_000),
         name="renew",
-    )(sector_sizes, term_shift, carried, site, keep)
+    )(sector_sizes, term_shift, upper, lower, turned, keep)
     applied = pl.pallas_call(
         finish_kernel,
         out_shape=jax.ShapeDtypeStruct((PIECE, WIDTH), F32),

time: 51.9 us -> 71.3 us (1.37)
  the two profiles are of different devices: /device:TPU:1 before, /device:TPU:32 now
where the time goes in v1:
time: 71.3 us; the launch traced here: 71.2 us
  waiting for transfers between devices  33.2 us (47%)
  starting transfers between devices  22.7 us (32%)
  Pallas kernels  9.89 us (14%)
  local copies, waits for them, and re-layouts  3.89 us (5%)
  between operations  1.48 us (2%)
    ppermute x13, waiting for transfers between devices, swap(): return lax.ppermute(block, ('term', 'sec'), route)  33.2 us
    ppermute x13, starting transfers between devices, swap(): return lax.ppermute(block, ('term', 'sec'), route)  22.7 us
    unnamed x12, local copies, waits for them, and re-layouts  3.89 us
    pallas_call x1, Pallas kernels, shards(): pl.pallas_call(renew_kernel, out_shape=(square, jax.ShapeDtypeStruct((8,...  2.4 us
    pallas_call x1, Pallas kernels, shards(): pl.pallas_call(prepare_kernel, out_shape=(square,) * 3, in_specs=[SMEM, S...  1.65 us
    pallas_call x1, Pallas kernels, shards(): pl.pallas_call(mix_kernel, out_shape=(square, strip), in_specs=[SMEM] + [...  1.51 us
  transfers between devices with their start and end apart: 13, of which 6 were waited for; matrix products, arithmetic and copies ran while one was open for 0% of the time, Pallas kernels for 12%

profile of v1, /device:TPU:32, one launch (start us, length us, event | category | flops | bytes accessed | tf_op | source)
XLA Modules:
  0.0 71.2 jit_solution(17986850732950755297)
XLA Ops:
  0.6 0.0 copy-start
  0.6 0.1 collective-permute-start
  0.7 0.0 copy-start.1
  0.8 1.3 %copy-done.1 = bf16[1,768,768]{2,1,0:T(8,128)(2,1)S(1)} copy-done((bf16[1,768,768]{2,1,0:T(8,128)(2,1)S(1)}, bf16[1,768,768]{2,1,0:T(8,128)(2,1)}, u32[]{:S(2)}) %copy-start.1) | copy-done | bytes 1179672
  2.1 0.0 copy-start.5
  2.1 0.6 cut.1
  2.7 3.9 %collective-permute-start.1 = (bf16[448,768]{1,0:T(8,128)(2,1)S(1)}, bf16[448,768]{1,0:T(8,128)(2,1)S(1)}, u32[]{:S(2)}, u32[]{:S(2)}) collective-permute-start(bf16[448,768]{1,0:T(8,128)(2,1)S(1)} %get-tuple-element.23), channel_id=1, source_target_pairs={{0,15},{1,2},{2,1},{3,4},{4,3},{5,6},{6,5},{7,8},{8,7},{9,10},{10,... | collective-permute-start | bytes 2064392 | tf_op jit(solution)/shard_map/ppermute | solution.py:41
  6.5 0.0 copy-done
  6.5 0.0 collective-permute-start.11
  6.5 0.9 %collective-permute-start.12 = (bf16[768,768]{1,0:T(8,128)(2,1)S(1)}, bf16[768,768]{1,0:T(8,128)(2,1)S(1)}, u32[]{:S(2)}, u32[]{:S(2)}) collective-permute-start(bf16[768,768]{1,0:T(8,128)(2,1)S(1)} %bitcast.7), channel_id=1, source_target_pairs={{0,15},{1,2},{2,1},{3,4},{4,3},{5,6},{6,5},{7,8},{8,7},{9,10},{10,... | collective-permute-start | bytes 3538952 | tf_op jit(solution)/shard_map/ppermute | solution.py:41
  7.5 2.9 %collective-permute-start.2 = (bf16[160,768]{1,0:T(8,128)(2,1)S(1)}, bf16[160,768]{1,0:T(8,128)(2,1)S(1)}, u32[]{:S(2)}, u32[]{:S(2)}) collective-permute-start(bf16[160,768]{1,0:T(8,128)(2,1)S(1)} %get-tuple-element.24), channel_id=1, source_target_pairs={{0,15},{1,2},{2,1},{3,4},{4,3},{5,6},{6,5},{7,8},{8,7},{9,10},{10,... | collective-permute-start | bytes 737288 | tf_op jit(solution)/shard_map/ppermute | solution.py:41
  10.4 20.1 %collective-permute-done.2.taken_ref = bf16[160,768]{1,0:T(8,128)(2,1)S(1)} collective-permute-done((bf16[160,768]{1,0:T(8,128)(2,1)S(1)}, bf16[160,768]{1,0:T(8,128)(2,1)S(1)}, u32[]{:S(2)}, u32[]{:S(2)}) %collective-permute-start.2) | collective-permute-done | bytes 245792 | tf_op jit(solution)/shard_map/ppermute | solution.py:41
  30.5 1.8 %collective-permute-start.3 = (bf16[160,768]{1,0:T(8,128)(2,1)S(1)}, bf16[160,768]{1,0:T(8,128)(2,1)S(1)}, u32[]{:S(2)}, u32[]{:S(2)}) collective-permute-start(bf16[160,768]{1,0:T(8,128)(2,1)S(1)} %collective-permute-done.2.taken_ref), channel_id=1, source_target_pairs={{0,32},{1,225},{2,34},{3,227},{4,36},{5,229},{6,38},{7,231},{8,40}... | collective-permute-start | bytes 737288 | tf_op jit(solution)/shard_map/ppermute | solution.py:41
  33.0 0.0 copy-done.5
  33.0 0.0 copy-start.3
  33.0 1.3 %copy-done.3 = bf16[1,1,768,768]{3,2,1,0:T(8,128)(2,1)S(1)} copy-done((bf16[1,1,768,768]{3,2,1,0:T(8,128)(2,1)S(1)}, bf16[1,1,768,768]{3,2,1,0:T(8,128)(2,1)}, u32[]{:S(2)}) %copy-start.3) | copy-done | bytes 1179672
  34.2 1.3 %copy-done.4 = bf16[1,1,768,768]{3,2,1,0:T(8,128)(2,1)S(1)} copy-done((bf16[1,1,768,768]{3,2,1,0:T(8,128)(2,1)S(1)}, bf16[1,1,768,768]{3,2,1,0:T(8,128)(2,1)}, u32[]{:S(2)}) %copy-start.4) | copy-done | bytes 1179672
  35.5 1.6 %prepare.1 = (bf16[768,768]{1,0:T(8,128)(2,1)S(1)}, bf16[768,768]{1,0:T(8,128)(2,1)S(1)}, bf16[768,768]{1,0:T(8,128)(2,1)S(1)}) custom-call(s32[16]{0:T(128)S(1)} %copy-done.5, s32[1]{0:T(128)S(6)} %copy.8.shift_ref, bf16[768,768]{1,0:T(8,128)(2,1)S(1)} %bitcast.14, bf16[768,768]{1,0:T(8,128)(2,1)S(1)} %bitcast.15, bf16[768,768]{1,0:T(8,128)(2,1)S(1)} %bitcast.8), custom_call_target="tpu_custom_call" | custom-call | flops 6000000 | bytes 1000 | tf_op jit(solution)/shard_map/prepare/pallas_call | solution.py:276
  37.2 0.0 copy-done.2
  37.2 0.6 bring.1
  37.8 0.0 collective-permute-done.3.passed_ref
  37.8 0.0 collective-permute-done.1.direct_ref
  37.8 0.0 collective-permute-done.pair_ref
  37.8 1.5 %mix.1 = (bf16[768,768]{1,0:T(8,128)(2,1)S(1)}, bf16[192,768]{1,0:T(8,128)(2,1)S(1)}) custom-call(s32[1]{0:T(128)S(6)} %copy.8.shift_ref, bf16[768,768]{1,0:T(8,128)(2,1)S(1)} %get-tuple-element.22.own_ref, bf16[768,768]{1,0:T(8,128)(2,1)S(1)} %collective-permute-done.pair_ref, bf16[448,768]{1,0:T(8,128)(2,1)S(1)} %collective-permute-done.1.direct_ref, ...), custom_call_target="tpu_custom_call" | custom-call | flops 1132462080 | bytes 6000000 | tf_op jit(solution)/shard_map/mix/pallas_call | solution.py:300
  39.3 0.8 %collective-permute-start.5 = (bf16[192,768]{1,0:T(8,128)(2,1)S(1)}, bf16[192,768]{1,0:T(8,128)(2,1)S(1)}, u32[]{:S(2)}, u32[]{:S(2)}) collective-permute-start(bf16[192,768]{1,0:T(8,128)(2,1)S(1)} %get-tuple-element.29), channel_id=1, source_target_pairs={{0,32},{1,225},{2,34},{3,227},{4,36},{5,229},{6,38},{7,231},{8,40}... | collective-permute-start | bytes 884744 | tf_op jit(solution)/shard_map/ppermute | solution.py:41
  40.1 0.4 send.1.after_ref
  40.5 1.4 %collective-permute-start.4 = (bf16[192,768]{1,0:T(8,128)(2,1)S(1)}, bf16[192,768]{1,0:T(8,128)(2,1)S(1)}, u32[]{:S(2)}, u32[]{:S(2)}) collective-permute-start(bf16[192,768]{1,0:T(8,128)(2,1)S(1)} %send.1.after_ref), channel_id=1, source_target_pairs={{0,32},{1,225},{2,34},{3,227},{4,36},{5,229},{6,38},{7,231},{8,40}... | collective-permute-start | bytes 884744 | tf_op jit(solution)/shard_map/ppermute | solution.py:41
  42.0 0.6 keep.1
  42.6 3.6 %collective-permute-done.5.got_ref = bf16[192,768]{1,0:T(8,128)(2,1)S(1)} collective-permute-done((bf16[192,768]{1,0:T(8,128)(2,1)S(1)}, bf16[192,768]{1,0:T(8,128)(2,1)S(1)}, u32[]{:S(2)}, u32[]{:S(2)}) %collective-permute-start.5) | collective-permute-done | bytes 294944 | tf_op jit(solution)/shard_map/ppermute | solution.py:41
  46.2 0.1 pass.1
  46.2 2.1 %collective-permute-start.6 = (bf16[144,768]{1,0:T(8,128)(2,1)S(1)}, bf16[144,768]{1,0:T(8,128)(2,1)S(1)}, u32[]{:S(2)}, u32[]{:S(2)}) collective-permute-start(bf16[144,768]{1,0:T(8,128)(2,1)S(1)} %get-tuple-element.30), channel_id=1, source_target_pairs={{0,224},{1,33},{2,226},{3,35},{4,228},{5,37},{6,230},{7,39},{8,232... | collective-permute-start | bytes 663560 | tf_op jit(solution)/shard_map/ppermute | solution.py:41
  48.3 0.1 collective-permute-start.7
  48.4 0.9 %collective-permute-done.4.got_ref = bf16[192,768]{1,0:T(8,128)(2,1)S(1)} collective-permute-done((bf16[192,768]{1,0:T(8,128)(2,1)S(1)}, bf16[192,768]{1,0:T(8,128)(2,1)S(1)}, u32[]{:S(2)}, u32[]{:S(2)}) %collective-permute-start.4) | collective-permute-done | bytes 294944 | tf_op jit(solution)/shard_map/ppermute | solution.py:41
  49.3 0.1 hold.1.hold_ref.after_ref
  49.4 0.0 collective-permute-done.11.pair_ref
  49.4 0.0 collective-permute-done.12.next_ref
  49.4 0.7 carry.2.upper_ref
  50.0 3.0 %collective-permute-done.7.got_ref = bf16[48,768]{1,0:T(8,128)(2,1)S(1)} collective-permute-done((bf16[48,768]{1,0:T(8,128)(2,1)S(1)}, bf16[48,768]{1,0:T(8,128)(2,1)S(1)}, u32[]{:S(2)}, u32[]{:S(2)}) %collective-permute-start.7) | collective-permute-done | bytes 73760 | tf_op jit(solution)/shard_map/ppermute | solution.py:41
  53.0 7.9 %collective-permute-start.8 = (bf16[48,768]{1,0:T(8,128)(2,1)S(1)}, bf16[48,768]{1,0:T(8,128)(2,1)S(1)}, u32[]{:S(2)}, u32[]{:S(2)}) collective-permute-start(bf16[48,768]{1,0:T(8,128)(2,1)S(1)} %split_first.1), channel_id=1, source_target_pairs={{0,112},{1,177},{2,114},{3,179},{4,116},{5,181},{6,118},{7,183},{8... | collective-permute-start | bytes 221192 | tf_op jit(solution)/shard_map/ppermute | solution.py:41
  61.0 0.0 collective-permute-done.6.got_ref
  61.0 0.4 collective-permute-start.10
  61.5 0.3 collective-permute-start.9
  61.7 0.6 carry.3.lower_ref
  62.3 2.4 %renew.1 = (bf16[768,768]{1,0:T(8,128)(2,1)}, f32[8,128]{1,0:T(8,128)S(1)}) custom-call(s32[16]{0:T(128)S(1)} %copy-done.5, s32[1]{0:T(128)S(6)} %copy.8.shift_ref, bf16[384,768]{1,0:T(8,128)(2,1)S(1)} %carry.2.upper_ref, bf16[384,768]{1,0:T(8,128)(2,1)S(1)} %carry.3.lower_ref, bf16[768,768]{1,0:T(8,128)(2,1)S(1)} %get-tuple-element.35.site_ref, ...), custom_call_target="tpu_custom_call" | custom-call | flops 905969664 | bytes 4000000 | tf_op jit(solution)/shard_map/renew/pallas_call | solution.py:387
  64.8 0.0 collective-permute-done.8.far_ref
  64.8 2.2 %collective-permute-done.10.half_ref = bf16[48,768]{1,0:T(8,128)(2,1)S(1)} collective-permute-done((bf16[48,768]{1,0:T(8,128)(2,1)S(1)}, bf16[48,768]{1,0:T(8,128)(2,1)S(1)}, u32[]{:S(2)}, u32[]{:S(2)}) %collective-permute-start.10) | collective-permute-done | bytes 73760 | tf_op jit(solution)/shard_map/ppermute | solution.py:41
  67.0 3.5 %collective-permute-done.9.ring_ref = bf16[48,768]{1,0:T(8,128)(2,1)S(1)} collective-permute-done((bf16[48,768]{1,0:T(8,128)(2,1)S(1)}, bf16[48,768]{1,0:T(8,128)(2,1)S(1)}, u32[]{:S(2)}, u32[]{:S(2)}) %collective-permute-start.9) | collective-permute-done | bytes 73760 | tf_op jit(solution)/shard_map/ppermute | solution.py:41
  70.5 0.7 finish.1
  (4 shorter events, 0.1 us)
Async XLA Ops:
  0.6 5.9 %copy-start = (bf16[1,768,768]{2,1,0:T(8,128)(2,1)S(1)}, bf16[1,768,768]{2,1,0:T(8,128)(2,1)}, u32[]{:S(2)}) copy-start(bf16[1,768,768]{2,1,0:T(8,128)(2,1)} %param.9) | copy-start | bytes 3538948
  0.6 37.2 %collective-permute-start = (bf16[768,768]{1,0:T(8,128)(2,1)}, bf16[768,768]{1,0:T(8,128)(2,1)S(1)}, u32[]{:S(2)}, u32[]{:S(2)}) collective-permute-start(bf16[768,768]{1,0:T(8,128)(2,1)} %bitcast.11), channel_id=1, source_target_pairs={{0,1},{1,0},{2,3},{3,2},{4,5},{5,4},{6,7},{7,6},{8,9},{9,8},{10,11... | collective-permute-start | bytes 3538952 | tf_op jit(solution)/shard_map/ppermute | solution.py:41
  0.7 1.3 %copy-start.1 = (bf16[1,768,768]{2,1,0:T(8,128)(2,1)S(1)}, bf16[1,768,768]{2,1,0:T(8,128)(2,1)}, u32[]{:S(2)}) copy-start(bf16[1,768,768]{2,1,0:T(8,128)(2,1)} %param.6) | copy-start | bytes 3538948
  2.1 30.9 %copy-start.5 = (s32[16]{0:T(128)S(1)}, s32[16]{0:T(128)}, u32[]{:S(2)}) copy-start(s32[16]{0:T(128)} %sizes_ref.3) | copy-start | bytes 196
  2.7 35.2 %collective-permute-start.1 = (bf16[448,768]{1,0:T(8,128)(2,1)S(1)}, bf16[448,768]{1,0:T(8,128)(2,1)S(1)}, u32[]{:S(2)}, u32[]{:S(2)}) collective-permute-start(bf16[448,768]{1,0:T(8,128)(2,1)S(1)} %get-tuple-element.23), channel_id=1, source_target_pairs={{0,15},{1,2},{2,1},{3,4},{4,3},{5,6},{6,5},{7,8},{8,7},{9,10},{10,... | collective-permute-start | bytes 2064392 | tf_op jit(solution)/shard_map/ppermute | solution.py:41
  6.5 42.8 %collective-permute-start.11 = (bf16[768,768]{1,0:T(8,128)(2,1)S(1)}, bf16[768,768]{1,0:T(8,128)(2,1)S(1)}, u32[]{:S(2)}, u32[]{:S(2)}) collective-permute-start(bf16[768,768]{1,0:T(8,128)(2,1)S(1)} %bitcast.6), channel_id=1, source_target_pairs={{0,1},{1,0},{2,3},{3,2},{4,5},{5,4},{6,7},{7,6},{8,9},{9,8},{10,11... | collective-permute-start | bytes 3538952 | tf_op jit(solution)/shard_map/ppermute | solution.py:41
  6.5 42.8 %collective-permute-start.12 = (bf16[768,768]{1,0:T(8,128)(2,1)S(1)}, bf16[768,768]{1,0:T(8,128)(2,1)S(1)}, u32[]{:S(2)}, u32[]{:S(2)}) collective-permute-start(bf16[768,768]{1,0:T(8,128)(2,1)S(1)} %bitcast.7), channel_id=1, source_target_pairs={{0,15},{1,2},{2,1},{3,4},{4,3},{5,6},{6,5},{7,8},{8,7},{9,10},{10,... | collective-permute-start | bytes 3538952 | tf_op jit(solution)/shard_map/ppermute | solution.py:41
  7.5 23.0 %collective-permute-start.2 = (bf16[160,768]{1,0:T(8,128)(2,1)S(1)}, bf16[160,768]{1,0:T(8,128)(2,1)S(1)}, u32[]{:S(2)}, u32[]{:S(2)}) collective-permute-start(bf16[160,768]{1,0:T(8,128)(2,1)S(1)} %get-tuple-element.24), channel_id=1, source_target_pairs={{0,15},{1,2},{2,1},{3,4},{4,3},{5,6},{6,5},{7,8},{8,7},{9,10},{10,... | collective-permute-start | bytes 737288 | tf_op jit(solution)/shard_map/ppermute | solution.py:41
  30.5 7.3 %collective-permute-start.3 = (bf16[160,768]{1,0:T(8,128)(2,1)S(1)}, bf16[160,768]{1,0:T(8,128)(2,1)S(1)}, u32[]{:S(2)}, u32[]{:S(2)}) collective-permute-start(bf16[160,768]{1,0:T(8,128)(2,1)S(1)} %collective-permute-done.2.taken_ref), channel_id=1, source_target_pairs={{0,32},{1,225},{2,34},{3,227},{4,36},{5,229},{6,38},{7,231},{8,40}... | collective-permute-start | bytes 737288 | tf_op jit(solution)/shard_map/ppermute | solution.py:41
  33.0 1.3 %copy-start.3 = (bf16[1,1,768,768]{3,2,1,0:T(8,128)(2,1)S(1)}, bf16[1,1,768,768]{3,2,1,0:T(8,128)(2,1)}, u32[]{:S(2)}) copy-start(bf16[1,1,768,768]{3,2,1,0:T(8,128)(2,1)} %param.7) | copy-start | bytes 3538948
  34.2 1.3 %copy-start.4 = (bf16[1,1,768,768]{3,2,1,0:T(8,128)(2,1)S(1)}, bf16[1,1,768,768]{3,2,1,0:T(8,128)(2,1)}, u32[]{:S(2)}) copy-start(bf16[1,1,768,768]{3,2,1,0:T(8,128)(2,1)} %param.8) | copy-start | bytes 3538948
  35.5 1.7 %copy-start.2 = (bf16[1,768,768]{2,1,0:T(8,128)(2,1)S(1)}, bf16[1,768,768]{2,1,0:T(8,128)(2,1)}, u32[]{:S(2)}) copy-start(bf16[1,768,768]{2,1,0:T(8,128)(2,1)} %param.6) | copy-start | bytes 3538948
  39.3 6.8 %collective-permute-start.5 = (bf16[192,768]{1,0:T(8,128)(2,1)S(1)}, bf16[192,768]{1,0:T(8,128)(2,1)S(1)}, u32[]{:S(2)}, u32[]{:S(2)}) collective-permute-start(bf16[192,768]{1,0:T(8,128)(2,1)S(1)} %get-tuple-element.29), channel_id=1, source_target_pairs={{0,32},{1,225},{2,34},{3,227},{4,36},{5,229},{6,38},{7,231},{8,40}... | collective-permute-start | bytes 884744 | tf_op jit(solution)/shard_map/ppermute | solution.py:41
  40.5 8.8 %collective-permute-start.4 = (bf16[192,768]{1,0:T(8,128)(2,1)S(1)}, bf16[192,768]{1,0:T(8,128)(2,1)S(1)}, u32[]{:S(2)}, u32[]{:S(2)}) collective-permute-start(bf16[192,768]{1,0:T(8,128)(2,1)S(1)} %send.1.after_ref), channel_id=1, source_target_pairs={{0,32},{1,225},{2,34},{3,227},{4,36},{5,229},{6,38},{7,231},{8,40}... | collective-permute-start | bytes 884744 | tf_op jit(solution)/shard_map/ppermute | solution.py:41
  46.2 14.8 %collective-permute-start.6 = (bf16[144,768]{1,0:T(8,128)(2,1)S(1)}, bf16[144,768]{1,0:T(8,128)(2,1)S(1)}, u32[]{:S(2)}, u32[]{:S(2)}) collective-permute-start(bf16[144,768]{1,0:T(8,128)(2,1)S(1)} %get-tuple-element.30), channel_id=1, source_target_pairs={{0,224},{1,33},{2,226},{3,35},{4,228},{5,37},{6,230},{7,39},{8,232... | collective-permute-start | bytes 663560 | tf_op jit(solution)/shard_map/ppermute | solution.py:41
  48.3 4.7 %collective-permute-start.7 = (bf16[48,768]{1,0:T(8,128)(2,1)S(1)}, bf16[48,768]{1,0:T(8,128)(2,1)S(1)}, u32[]{:S(2)}, u32[]{:S(2)}) collective-permute-start(bf16[48,768]{1,0:T(8,128)(2,1)S(1)} %get-tuple-element.32), channel_id=1, source_target_pairs={{0,224},{1,33},{2,226},{3,35},{4,228},{5,37},{6,230},{7,39},{8,232... | collective-permute-start | bytes 221192 | tf_op jit(solution)/shard_map/ppermute | solution.py:41
  53.0 11.7 %collective-permute-start.8 = (bf16[48,768]{1,0:T(8,128)(2,1)S(1)}, bf16[48,768]{1,0:T(8,128)(2,1)S(1)}, u32[]{:S(2)}, u32[]{:S(2)}) collective-permute-start(bf16[48,768]{1,0:T(8,128)(2,1)S(1)} %split_first.1), channel_id=1, source_target_pairs={{0,112},{1,177},{2,114},{3,179},{4,116},{5,181},{6,118},{7,183},{8... | collective-permute-start | bytes 221192 | tf_op jit(solution)/shard_map/ppermute | solution.py:41
  61.0 5.9 %collective-permute-start.10 = (bf16[48,768]{1,0:T(8,128)(2,1)S(1)}, bf16[48,768]{1,0:T(8,128)(2,1)S(1)}, u32[]{:S(2)}, u32[]{:S(2)}) collective-permute-start(bf16[48,768]{1,0:T(8,128)(2,1)S(1)} %get-tuple-element.34), channel_id=1, source_target_pairs={{0,16},{1,17},{2,18},{3,19},{4,20},{5,21},{6,22},{7,23},{8,24},{9,... | collective-permute-start | bytes 221192 | tf_op jit(solution)/shard_map/ppermute | solution.py:41
  61.5 9.0 %collective-permute-start.9 = (bf16[48,768]{1,0:T(8,128)(2,1)S(1)}, bf16[48,768]{1,0:T(8,128)(2,1)S(1)}, u32[]{:S(2)}, u32[]{:S(2)}) collective-permute-start(bf16[48,768]{1,0:T(8,128)(2,1)S(1)} %get-tuple-element.33), channel_id=1, source_target_pairs={{0,96},{1,161},{2,98},{3,163},{4,100},{5,165},{6,102},{7,167},{8,1... | collective-permute-start | bytes 221192 | tf_op jit(solution)/shard_map/ppermute | solution.py:41

commit v2 on v1

--- a/solution.py
+++ b/solution.py
@@ -13,6 +13,7 @@
 SECTORS = 16
 PIECE = WIDTH // TERMS
 QUARTER = WIDTH // 4
+SLOTS = (0, 4, 1, 2, 3, 5, 6, 7, 8, 9, 10, 11, 12, 13, 14, 15)
 RELAYED = 160
 DIRECT = WIDTH - 2 * RELAYED
 RINGS = TERMS // 2
@@ -129,13 +130,13 @@
     source_columns = ones_below(source, 0, WIDTH, 1)
     for copy in copies:
         copy.wait()
-    for slot in range(TERMS):
+    for place, slot in enumerate(SLOTS):
         start = pl.multiple_of(piece_at(slot) * PIECE, 16)
-        here = pl.ds(slot * PIECE, PIECE)
+        here = pl.ds(place * PIECE, PIECE)
         rows = ones_below(own, start, PIECE, 0)
         left_out[here, :] = left_ref[pl.ds(start, PIECE), :] * rows * source_columns
         site_out[here, :] = site_ref[pl.ds(start, PIECE), :] * own_columns
-        source_rows = ones_below(source, slot * PIECE, PIECE, 0)
+        source_rows = ones_below(source, place * PIECE, PIECE, 0)
         right_out[here, :] = right_ref[here, :] * source_rows * own_columns
 
 
@@ -160,13 +161,16 @@
     right_ref,
     left_ref,
     mixed_out,
+    lead_out,
     send_out,
     joined_ref,
 ):
     def body(source_ref):
         mixed = jnp.dot(source_ref[...], right_ref[...], preferred_element_type=F32).astype(BF16)
         mixed_out[...] = mixed
-        send_out[...] = jnp.dot(left_ref[:QUARTER, :], mixed, preferred_element_type=F32).astype(BF16)
+        send = jnp.dot(left_ref[: 5 * PIECE, :], mixed, preferred_element_type=F32).astype(BF16)
+        lead_out[...] = send[: 2 * PIECE, :]
+        send_out[...] = send[2 * PIECE :, :]
 
     def joined():
         taken, passed = relay_starts()
@@ -179,7 +183,7 @@
 
 
 def send_kernel(left_ref, mixed_ref, send_out):
-    rows = left_ref[QUARTER : 2 * QUARTER, :]
+    rows = left_ref[5 * PIECE : 8 * PIECE, :]
     send_out[...] = jnp.dot(rows, mixed_ref[...], preferred_element_type=F32).astype(BF16)
 
 
@@ -190,19 +194,24 @@
         out[...] = jnp.dot(rows, mixed_ref[...], preferred_element_type=F32)
 
 
-def pass_kernel(keep_ref, got_ref, first_out, second_out):
-    for here, out in ((pl.ds(0, PIECE), first_out), (pl.ds(PIECE, 3 * PIECE), second_out)):
-        out[...] = (keep_ref[here, :] + got_ref[here, :].astype(F32)).astype(BF16)
+def pass_kernel(start, keep_ref, got_ref, out_ref):
+    here = pl.ds(start, out_ref.shape[0])
+    out_ref[...] = (keep_ref[here, :] + got_ref[: out_ref.shape[0], :].astype(F32)).astype(BF16)
 
 
 def hold_kernel(keep_ref, got_ref, out_ref):
-    out_ref[...] = keep_ref[...] + got_ref[...].astype(F32)
-
-
-def split_kernel(start, hold_ref, got_ref, *outs):
+    out_ref[...] = keep_ref[PIECE:, :] + got_ref[...].astype(F32)
+
+
+def far_kernel(keep_ref, lead_ref, moved_ref, out_ref):
+    total = keep_ref[:PIECE, :] + lead_ref[PIECE:, :].astype(F32) + moved_ref[...].astype(F32)
+    out_ref[...] = total.astype(BF16)
+
+
+def split_kernel(hold_ref, got_ref, *outs):
     for slot, out in enumerate(outs):
-        mine, theirs = pl.ds((start + slot) * PIECE, PIECE), pl.ds(slot * PIECE, PIECE)
-        out[...] = (hold_ref[mine, :] + got_ref[theirs, :].astype(F32)).astype(out.dtype)
+        here = pl.ds(slot * PIECE, PIECE)
+        out[...] = (hold_ref[here, :] + got_ref[here, :].astype(F32)).astype(out.dtype)
 
 
 def finish_kernel(keep_ref, far_ref, ring_ref, half_ref, done_ref, out_ref):
@@ -294,23 +303,25 @@
         name="bring",
     )(state_own, site)
     anywhere = pl.BlockSpec(memory_space=pl.ANY)
-    strip = jax.ShapeDtypeStruct((QUARTER, WIDTH), BF16)
     strip_sum = jax.ShapeDtypeStruct((QUARTER, WIDTH), F32)
+    piece = jax.ShapeDtypeStruct((PIECE, WIDTH), BF16)
+    pieces = jax.ShapeDtypeStruct((3 * PIECE, WIDTH), BF16)
     strip_flops = 2 * QUARTER * WIDTH * WIDTH
-    mixed, send_first = pl.pallas_call(
+    mixed, send_lead, send_first = pl.pallas_call(
         mix_kernel,
-        out_shape=(square, strip),
+        out_shape=(square, jax.ShapeDtypeStruct((2 * PIECE, WIDTH), BF16), pieces),
         in_specs=[SMEM] + [VMEM] * 7,
-        out_specs=(VMEM, VMEM),
+        out_specs=(VMEM, VMEM, VMEM),
         scratch_shapes=[pltpu.VMEM((WIDTH, WIDTH), BF16)],
         compiler_params=room(20),
         cost_estimate=cost(5 * strip_flops, 6_000_000),
         name="mix",
     )(term_shift, state_here, state_pair, direct_got, taken, passed, right, left)
+    got_lead = swap(send_lead, stage_route(0))
     got_first = swap(send_first, stage_route(0))
     send_second = pl.pallas_call(
         send_kernel,
-        out_shape=strip,
+        out_shape=pieces,
         in_specs=[VMEM, VMEM],
         out_specs=VMEM,
         compiler_params=room(12),
@@ -327,22 +338,25 @@
         cost_estimate=cost(2 * strip_flops, 3_000_000),
         name="keep",
     )(left, mixed, send_second)
-    piece = jax.ShapeDtypeStruct((PIECE, WIDTH), BF16)
-    pieces = jax.ShapeDtypeStruct((3 * PIECE, WIDTH), BF16)
-    pass_first, pass_second = pl.pallas_call(
-        pass_kernel,
-        out_shape=(piece, pieces),
-        in_specs=[VMEM, VMEM],
-        out_specs=(VMEM, VMEM),
-        compiler_params=room(6),
-        cost_estimate=cost(QUARTER * WIDTH, 8 * QUARTER * WIDTH),
-        name="pass",
-    )(keep_first, got_first)
+
+    def passing(start, got, shape):
+        return pl.pallas_call(
+            functools.partial(pass_kernel, start),
+            out_shape=shape,
+            in_specs=[VMEM, VMEM],
+            out_specs=VMEM,
+            compiler_params=room(6),
+            cost_estimate=cost(QUARTER * WIDTH, 8 * QUARTER * WIDTH),
+            name="pass",
+        )(keep_first, got)
+
+    pass_first = passing(0, got_lead, piece)
     moved_first = swap(pass_first, stage_route(1))
+    pass_second = passing(PIECE, got_first, pieces)
     moved_second = swap(pass_second, stage_route(1))
     held = pl.pallas_call(
         hold_kernel,
-        out_shape=strip_sum,
+        out_shape=jax.ShapeDtypeStruct((3 * PIECE, WIDTH), F32),
         in_specs=[VMEM, VMEM],
         out_specs=VMEM,
         compiler_params=room(6),
@@ -361,19 +375,19 @@
             name="carry",
         )(term_shift, site_own, site_pair, site_next, left, after)
 
-    upper = carry(0, held)
-    (far,) = pl.pallas_call(
-        functools.partial(split_kernel, 0),
-        out_shape=(piece,),
-        in_specs=[VMEM, VMEM],
-        out_specs=(VMEM,),
+    far = pl.pallas_call(
+        far_kernel,
+        out_shape=piece,
+        in_specs=[VMEM] * 3,
+        out_specs=VMEM,
         compiler_params=room(6),
         cost_estimate=cost(PIECE * WIDTH, 8 * PIECE * WIDTH),
-        name="split_first",
-    )(held, moved_first)
+        name="far",
+    )(keep_second, got_lead, moved_first)
     far_got = swap(far, far_route)
+    upper = carry(0, far)
     ring, half, keep = pl.pallas_call(
-        functools.partial(split_kernel, 1),
+        split_kernel,
         out_shape=(piece, piece, jax.ShapeDtypeStruct((PIECE, WIDTH), F32)),
         in_specs=[VMEM, VMEM],
         out_specs=(VMEM, VMEM, VMEM),

time: 71.3 us -> 71.4 us (level)
  the two profiles are of different devices: /device:TPU:32 before, /device:TPU:7 now
where the time goes in v2:
time: 71.4 us; the launch traced here: 71.2 us
  waiting for transfers between devices  33.2 us (46%)
  starting transfers between devices  22.5 us (32%)
  Pallas kernels  10.2 us (14%)
  local copies, waits for them, and re-layouts  3.82 us (5%)
  between operations  1.49 us (2%)
    ppermute x14, waiting for transfers between devices, swap(): return lax.ppermute(block, ('term', 'sec'), route)  33.2 us
    ppermute x14, starting transfers between devices, swap(): return lax.ppermute(block, ('term', 'sec'), route)  22.5 us
    unnamed x12, local copies, waits for them, and re-layouts  3.82 us
    pallas_call x1, Pallas kernels, shards(): pl.pallas_call(renew_kernel, out_shape=(square, jax.ShapeDtypeStruct((8,...  2.46 us
    pallas_call x1, Pallas kernels, shards(): pl.pallas_call(prepare_kernel, out_shape=(square,) * 3, in_specs=[SMEM, S...  1.66 us
    pallas_call x1, Pallas kernels, shards(): pl.pallas_call(mix_kernel, out_shape=(square, jax.ShapeDtypeStruct((2 * P...  1.59 us
    pallas_call x2, Pallas kernels, carry(): pl.pallas_call(functools.partial(carry_kernel, part), out_shape=jax.Shape...  1.47 us
  transfers between devices with their start and end apart: 14, of which 5 were waited for; matrix products, arithmetic and copies ran while one was open for 0% of the time, Pallas kernels for 13%

profile of v2, /device:TPU:7, one launch (start us, length us, event | category | flops | bytes accessed | tf_op | source)
XLA Modules:
  0.0 71.2 jit_solution(2339039284207152910)
XLA Ops:
  0.6 0.0 copy-start
  0.6 0.8 %collective-permute-start = (bf16[768,768]{1,0:T(8,128)(2,1)}, bf16[768,768]{1,0:T(8,128)(2,1)S(1)}, u32[]{:S(2)}, u32[]{:S(2)}) collective-permute-start(bf16[768,768]{1,0:T(8,128)(2,1)} %bitcast.11), channel_id=1, source_target_pairs={{0,1},{1,0},{2,3},{3,2},{4,5},{5,4},{6,7},{7,6},{8,9},{9,8},{10,11... | collective-permute-start | bytes 3538952 | tf_op jit(solution)/shard_map/ppermute | solution.py:42
  1.4 1.3 %copy-done.1 = bf16[1,768,768]{2,1,0:T(8,128)(2,1)S(1)} copy-done((bf16[1,768,768]{2,1,0:T(8,128)(2,1)S(1)}, bf16[1,768,768]{2,1,0:T(8,128)(2,1)}, u32[]{:S(2)}) %copy-start.1) | copy-done | bytes 1179672
  2.7 0.6 cut.1
  3.2 1.3 %collective-permute-start.1 = (bf16[448,768]{1,0:T(8,128)(2,1)S(1)}, bf16[448,768]{1,0:T(8,128)(2,1)S(1)}, u32[]{:S(2)}, u32[]{:S(2)}) collective-permute-start(bf16[448,768]{1,0:T(8,128)(2,1)S(1)} %get-tuple-element.22), channel_id=1, source_target_pairs={{0,15},{1,2},{2,1},{3,4},{4,3},{5,6},{6,5},{7,8},{8,7},{9,10},{10,... | collective-permute-start | bytes 2064392 | tf_op jit(solution)/shard_map/ppermute | solution.py:42
  4.5 0.0 copy-done
  4.5 0.0 collective-permute-start.12
  4.5 2.7 %collective-permute-start.13 = (bf16[768,768]{1,0:T(8,128)(2,1)S(1)}, bf16[768,768]{1,0:T(8,128)(2,1)S(1)}, u32[]{:S(2)}, u32[]{:S(2)}) collective-permute-start(bf16[768,768]{1,0:T(8,128)(2,1)S(1)} %bitcast.7), channel_id=1, source_target_pairs={{0,15},{1,2},{2,1},{3,4},{4,3},{5,6},{6,5},{7,8},{8,7},{9,10},{10,... | collective-permute-start | bytes 3538952 | tf_op jit(solution)/shard_map/ppermute | solution.py:42
  7.2 1.2 %collective-permute-start.2 = (bf16[160,768]{1,0:T(8,128)(2,1)S(1)}, bf16[160,768]{1,0:T(8,128)(2,1)S(1)}, u32[]{:S(2)}, u32[]{:S(2)}) collective-permute-start(bf16[160,768]{1,0:T(8,128)(2,1)S(1)} %get-tuple-element.23), channel_id=1, source_target_pairs={{0,15},{1,2},{2,1},{3,4},{4,3},{5,6},{6,5},{7,8},{8,7},{9,10},{10,... | collective-permute-start | bytes 737288 | tf_op jit(solution)/shard_map/ppermute | solution.py:42
  8.4 22.7 %collective-permute-done.2.taken_ref = bf16[160,768]{1,0:T(8,128)(2,1)S(1)} collective-permute-done((bf16[160,768]{1,0:T(8,128)(2,1)S(1)}, bf16[160,768]{1,0:T(8,128)(2,1)S(1)}, u32[]{:S(2)}, u32[]{:S(2)}) %collective-permute-start.2) | collective-permute-done | bytes 245792 | tf_op jit(solution)/shard_map/ppermute | solution.py:42
  31.1 5.6 %collective-permute-start.3 = (bf16[160,768]{1,0:T(8,128)(2,1)S(1)}, bf16[160,768]{1,0:T(8,128)(2,1)S(1)}, u32[]{:S(2)}, u32[]{:S(2)}) collective-permute-start(bf16[160,768]{1,0:T(8,128)(2,1)S(1)} %collective-permute-done.2.taken_ref), channel_id=1, source_target_pairs={{0,32},{1,225},{2,34},{3,227},{4,36},{5,229},{6,38},{7,231},{8,40}... | collective-permute-start | bytes 737288 | tf_op jit(solution)/shard_map/ppermute | solution.py:42
  37.3 0.0 copy-done.5
  37.3 0.0 copy-start.3
  37.3 1.3 %copy-done.3 = bf16[1,1,768,768]{3,2,1,0:T(8,128)(2,1)S(1)} copy-done((bf16[1,1,768,768]{3,2,1,0:T(8,128)(2,1)S(1)}, bf16[1,1,768,768]{3,2,1,0:T(8,128)(2,1)}, u32[]{:S(2)}) %copy-start.3) | copy-done | bytes 1179672
  38.6 1.3 %copy-done.4 = bf16[1,1,768,768]{3,2,1,0:T(8,128)(2,1)S(1)} copy-done((bf16[1,1,768,768]{3,2,1,0:T(8,128)(2,1)S(1)}, bf16[1,1,768,768]{3,2,1,0:T(8,128)(2,1)}, u32[]{:S(2)}) %copy-start.4) | copy-done | bytes 1179672
  39.9 1.7 %prepare.1 = (bf16[768,768]{1,0:T(8,128)(2,1)S(1)}, bf16[768,768]{1,0:T(8,128)(2,1)S(1)}, bf16[768,768]{1,0:T(8,128)(2,1)S(1)}) custom-call(s32[16]{0:T(128)S(1)} %copy-done.5, s32[1]{0:T(128)S(6)} %copy.8.shift_ref, bf16[768,768]{1,0:T(8,128)(2,1)S(1)} %bitcast.14, bf16[768,768]{1,0:T(8,128)(2,1)S(1)} %bitcast.15, bf16[768,768]{1,0:T(8,128)(2,1)S(1)} %bitcast.8), custom_call_target="tpu_custom_call" | custom-call | flops 6000000 | bytes 1000 | tf_op jit(solution)/shard_map/prepare/pallas_call | solution.py:285
  41.5 0.0 copy-done.2
  41.5 0.6 bring.1
  42.1 0.0 collective-permute-done.3.passed_ref
  42.2 0.0 collective-permute-done.1.direct_ref
  42.2 0.0 collective-permute-done.pair_ref
  42.2 1.6 %mix.1 = (bf16[768,768]{1,0:T(8,128)(2,1)S(1)}, bf16[96,768]{1,0:T(8,128)(2,1)S(1)}, bf16[144,768]{1,0:T(8,128)(2,1)S(1)}) custom-call(s32[1]{0:T(128)S(6)} %copy.8.shift_ref, bf16[768,768]{1,0:T(8,128)(2,1)S(1)} %get-tuple-element.21.own_ref, bf16[768,768]{1,0:T(8,128)(2,1)S(1)} %collective-permute-done.pair_ref, ...), custom_call_target="tpu_custom_call" | custom-call | flops 1132462080 | bytes 6000000 | tf_op jit(solution)/shard_map/mix/pallas_call | solution.py:310
  43.8 0.8 %collective-permute-start.5 = (bf16[144,768]{1,0:T(8,128)(2,1)S(1)}, bf16[144,768]{1,0:T(8,128)(2,1)S(1)}, u32[]{:S(2)}, u32[]{:S(2)}) collective-permute-start(bf16[144,768]{1,0:T(8,128)(2,1)S(1)} %get-tuple-element.28), channel_id=1, source_target_pairs={{0,32},{1,225},{2,34},{3,227},{4,36},{5,229},{6,38},{7,231},{8,40}... | collective-permute-start | bytes 663560 | tf_op jit(solution)/shard_map/ppermute | solution.py:42
  44.6 2.0 %collective-permute-start.7 = (bf16[96,768]{1,0:T(8,128)(2,1)S(1)}, bf16[96,768]{1,0:T(8,128)(2,1)S(1)}, u32[]{:S(2)}, u32[]{:S(2)}) collective-permute-start(bf16[96,768]{1,0:T(8,128)(2,1)S(1)} %get-tuple-element.30), channel_id=1, source_target_pairs={{0,32},{1,225},{2,34},{3,227},{4,36},{5,229},{6,38},{7,231},{8,40}... | collective-permute-start | bytes 442376 | tf_op jit(solution)/shard_map/ppermute | solution.py:42
  46.5 0.3 send.1.after_ref
  46.9 0.8 %collective-permute-start.4 = (bf16[144,768]{1,0:T(8,128)(2,1)S(1)}, bf16[144,768]{1,0:T(8,128)(2,1)S(1)}, u32[]{:S(2)}, u32[]{:S(2)}) collective-permute-start(bf16[144,768]{1,0:T(8,128)(2,1)S(1)} %send.1.after_ref), channel_id=1, source_target_pairs={{0,32},{1,225},{2,34},{3,227},{4,36},{5,229},{6,38},{7,231},{8,40}... | collective-permute-start | bytes 663560 | tf_op jit(solution)/shard_map/ppermute | solution.py:42
  47.7 0.6 keep.1
  48.3 1.5 %collective-permute-done.5.got_ref = bf16[144,768]{1,0:T(8,128)(2,1)S(1)} collective-permute-done((bf16[144,768]{1,0:T(8,128)(2,1)S(1)}, bf16[144,768]{1,0:T(8,128)(2,1)S(1)}, u32[]{:S(2)}, u32[]{:S(2)}) %collective-permute-start.5) | collective-permute-done | bytes 221216 | tf_op jit(solution)/shard_map/ppermute | solution.py:42
  49.9 0.1 pass.2
  49.9 0.1 collective-permute-start.6
  50.0 3.1 %collective-permute-done.7.got_ref.lead_ref = bf16[96,768]{1,0:T(8,128)(2,1)S(1)} collective-permute-done((bf16[96,768]{1,0:T(8,128)(2,1)S(1)}, bf16[96,768]{1,0:T(8,128)(2,1)S(1)}, u32[]{:S(2)}, u32[]{:S(2)}) %collective-permute-start.7) | collective-permute-done | bytes 147488 | tf_op jit(solution)/shard_map/ppermute | solution.py:42
  53.1 0.1 collective-permute-start.8
  53.2 3.4 %collective-permute-done.8.moved_ref = bf16[48,768]{1,0:T(8,128)(2,1)S(1)} collective-permute-done((bf16[48,768]{1,0:T(8,128)(2,1)S(1)}, bf16[48,768]{1,0:T(8,128)(2,1)S(1)}, u32[]{:S(2)}, u32[]{:S(2)}) %collective-permute-start.8) | collective-permute-done | bytes 73760 | tf_op jit(solution)/shard_map/ppermute | solution.py:42
  56.7 2.8 %collective-permute-start.9 = (bf16[48,768]{1,0:T(8,128)(2,1)S(1)}, bf16[48,768]{1,0:T(8,128)(2,1)S(1)}, u32[]{:S(2)}, u32[]{:S(2)}) collective-permute-start(bf16[48,768]{1,0:T(8,128)(2,1)S(1)} %far.1.after_ref), channel_id=1, source_target_pairs={{0,112},{1,177},{2,114},{3,179},{4,116},{5,181},{6,118},{7,183},{8... | collective-permute-start | bytes 221192 | tf_op jit(solution)/shard_map/ppermute | solution.py:42
  59.5 0.0 collective-permute-done.4.got_ref
  59.5 0.0 collective-permute-done.12.pair_ref
  59.6 0.0 collective-permute-done.13.next_ref
  59.6 0.8 %carry.2.upper_ref = bf16[384,768]{1,0:T(8,128)(2,1)S(1)} custom-call(s32[1]{0:T(128)S(6)} %copy.8.shift_ref, bf16[768,768]{1,0:T(8,128)(2,1)S(1)} %bitcast.9, bf16[768,768]{1,0:T(8,128)(2,1)S(1)} %collective-permute-done.12.pair_ref, bf16[768,768]{1,0:T(8,128)(2,1)S(1)} %collective-permute-done.13.next_ref, ...), custom_call_target="tpu_custom_call" | custom-call | flops 452984832 | bytes 4000000 | tf_op jit(solution)/shard_map/carry/pallas_call | solution.py:368
  60.4 0.0 collective-permute-done.6.got_ref
  60.4 0.1 split_second.1
  60.5 4.5 %collective-permute-start.10 = (bf16[48,768]{1,0:T(8,128)(2,1)S(1)}, bf16[48,768]{1,0:T(8,128)(2,1)S(1)}, u32[]{:S(2)}, u32[]{:S(2)}) collective-permute-start(bf16[48,768]{1,0:T(8,128)(2,1)S(1)} %get-tuple-element.31), channel_id=1, source_target_pairs={{0,96},{1,161},{2,98},{3,163},{4,100},{5,165},{6,102},{7,167},{8,1... | collective-permute-start | bytes 221192 | tf_op jit(solution)/shard_map/ppermute | solution.py:42
  65.0 0.1 collective-permute-start.11
  65.0 0.6 carry.3.lower_ref
  65.7 2.5 %renew.1 = (bf16[768,768]{1,0:T(8,128)(2,1)}, f32[8,128]{1,0:T(8,128)S(1)}) custom-call(s32[16]{0:T(128)S(1)} %copy-done.5, s32[1]{0:T(128)S(6)} %copy.8.shift_ref, bf16[384,768]{1,0:T(8,128)(2,1)S(1)} %carry.2.upper_ref, bf16[384,768]{1,0:T(8,128)(2,1)S(1)} %carry.3.lower_ref, bf16[768,768]{1,0:T(8,128)(2,1)S(1)} %get-tuple-element.33.site_ref, ...), custom_call_target="tpu_custom_call" | custom-call | flops 905969664 | bytes 4000000 | tf_op jit(solution)/shard_map/renew/pallas_call | solution.py:401
  68.1 0.0 collective-permute-done.9.far_ref
  68.1 0.0 collective-permute-done.10.ring_ref
  68.2 2.4 %collective-permute-done.11.half_ref = bf16[48,768]{1,0:T(8,128)(2,1)S(1)} collective-permute-done((bf16[48,768]{1,0:T(8,128)(2,1)S(1)}, bf16[48,768]{1,0:T(8,128)(2,1)S(1)}, u32[]{:S(2)}, u32[]{:S(2)}) %collective-permute-start.11) | collective-permute-done | bytes 73760 | tf_op jit(solution)/shard_map/ppermute | solution.py:42
  70.5 0.7 finish.1
  (7 shorter events, 0.1 us)
Async XLA Ops:
  0.6 3.9 %copy-start = (bf16[1,768,768]{2,1,0:T(8,128)(2,1)S(1)}, bf16[1,768,768]{2,1,0:T(8,128)(2,1)}, u32[]{:S(2)}) copy-start(bf16[1,768,768]{2,1,0:T(8,128)(2,1)} %param.9) | copy-start | bytes 3538948
  0.6 41.5 %collective-permute-start = (bf16[768,768]{1,0:T(8,128)(2,1)}, bf16[768,768]{1,0:T(8,128)(2,1)S(1)}, u32[]{:S(2)}, u32[]{:S(2)}) collective-permute-start(bf16[768,768]{1,0:T(8,128)(2,1)} %bitcast.11), channel_id=1, source_target_pairs={{0,1},{1,0},{2,3},{3,2},{4,5},{5,4},{6,7},{7,6},{8,9},{9,8},{10,11... | collective-permute-start | bytes 3538952 | tf_op jit(solution)/shard_map/ppermute | solution.py:42
  1.4 1.3 %copy-start.1 = (bf16[1,768,768]{2,1,0:T(8,128)(2,1)S(1)}, bf16[1,768,768]{2,1,0:T(8,128)(2,1)}, u32[]{:S(2)}) copy-start(bf16[1,768,768]{2,1,0:T(8,128)(2,1)} %param.6) | copy-start | bytes 3538948
  2.7 34.6 %copy-start.5 = (s32[16]{0:T(128)S(1)}, s32[16]{0:T(128)}, u32[]{:S(2)}) copy-start(s32[16]{0:T(128)} %sizes_ref.3) | copy-start | bytes 196
  3.2 38.9 %collective-permute-start.1 = (bf16[448,768]{1,0:T(8,128)(2,1)S(1)}, bf16[448,768]{1,0:T(8,128)(2,1)S(1)}, u32[]{:S(2)}, u32[]{:S(2)}) collective-permute-start(bf16[448,768]{1,0:T(8,128)(2,1)S(1)} %get-tuple-element.22), channel_id=1, source_target_pairs={{0,15},{1,2},{2,1},{3,4},{4,3},{5,6},{6,5},{7,8},{8,7},{9,10},{10,... | collective-permute-start | bytes 2064392 | tf_op jit(solution)/shard_map/ppermute | solution.py:42
  4.5 55.0 %collective-permute-start.12 = (bf16[768,768]{1,0:T(8,128)(2,1)S(1)}, bf16[768,768]{1,0:T(8,128)(2,1)S(1)}, u32[]{:S(2)}, u32[]{:S(2)}) collective-permute-start(bf16[768,768]{1,0:T(8,128)(2,1)S(1)} %bitcast.6), channel_id=1, source_target_pairs={{0,1},{1,0},{2,3},{3,2},{4,5},{5,4},{6,7},{7,6},{8,9},{9,8},{10,11... | collective-permute-start | bytes 3538952 | tf_op jit(solution)/shard_map/ppermute | solution.py:42
  4.5 55.0 %collective-permute-start.13 = (bf16[768,768]{1,0:T(8,128)(2,1)S(1)}, bf16[768,768]{1,0:T(8,128)(2,1)S(1)}, u32[]{:S(2)}, u32[]{:S(2)}) collective-permute-start(bf16[768,768]{1,0:T(8,128)(2,1)S(1)} %bitcast.7), channel_id=1, source_target_pairs={{0,15},{1,2},{2,1},{3,4},{4,3},{5,6},{6,5},{7,8},{8,7},{9,10},{10,... | collective-permute-start | bytes 3538952 | tf_op jit(solution)/shard_map/ppermute | solution.py:42
  7.2 23.9 %collective-permute-start.2 = (bf16[160,768]{1,0:T(8,128)(2,1)S(1)}, bf16[160,768]{1,0:T(8,128)(2,1)S(1)}, u32[]{:S(2)}, u32[]{:S(2)}) collective-permute-start(bf16[160,768]{1,0:T(8,128)(2,1)S(1)} %get-tuple-element.23), channel_id=1, source_target_pairs={{0,15},{1,2},{2,1},{3,4},{4,3},{5,6},{6,5},{7,8},{8,7},{9,10},{10,... | collective-permute-start | bytes 737288 | tf_op jit(solution)/shard_map/ppermute | solution.py:42
  31.1 11.1 %collective-permute-start.3 = (bf16[160,768]{1,0:T(8,128)(2,1)S(1)}, bf16[160,768]{1,0:T(8,128)(2,1)S(1)}, u32[]{:S(2)}, u32[]{:S(2)}) collective-permute-start(bf16[160,768]{1,0:T(8,128)(2,1)S(1)} %collective-permute-done.2.taken_ref), channel_id=1, source_target_pairs={{0,32},{1,225},{2,34},{3,227},{4,36},{5,229},{6,38},{7,231},{8,40}... | collective-permute-start | bytes 737288 | tf_op jit(solution)/shard_map/ppermute | solution.py:42
  37.3 1.3 %copy-start.3 = (bf16[1,1,768,768]{3,2,1,0:T(8,128)(2,1)S(1)}, bf16[1,1,768,768]{3,2,1,0:T(8,128)(2,1)}, u32[]{:S(2)}) copy-start(bf16[1,1,768,768]{3,2,1,0:T(8,128)(2,1)} %param.7) | copy-start | bytes 3538948
  38.6 1.3 %copy-start.4 = (bf16[1,1,768,768]{3,2,1,0:T(8,128)(2,1)S(1)}, bf16[1,1,768,768]{3,2,1,0:T(8,128)(2,1)}, u32[]{:S(2)}) copy-start(bf16[1,1,768,768]{3,2,1,0:T(8,128)(2,1)} %param.8) | copy-start | bytes 3538948
  39.9 1.7 %copy-start.2 = (bf16[1,768,768]{2,1,0:T(8,128)(2,1)S(1)}, bf16[1,768,768]{2,1,0:T(8,128)(2,1)}, u32[]{:S(2)}) copy-start(bf16[1,768,768]{2,1,0:T(8,128)(2,1)} %param.6) | copy-start | bytes 3538948
  43.8 6.1 %collective-permute-start.5 = (bf16[144,768]{1,0:T(8,128)(2,1)S(1)}, bf16[144,768]{1,0:T(8,128)(2,1)S(1)}, u32[]{:S(2)}, u32[]{:S(2)}) collective-permute-start(bf16[144,768]{1,0:T(8,128)(2,1)S(1)} %get-tuple-element.28), channel_id=1, source_target_pairs={{0,32},{1,225},{2,34},{3,227},{4,36},{5,229},{6,38},{7,231},{8,40}... | collective-permute-start | bytes 663560 | tf_op jit(solution)/shard_map/ppermute | solution.py:42
  44.6 8.5 %collective-permute-start.7 = (bf16[96,768]{1,0:T(8,128)(2,1)S(1)}, bf16[96,768]{1,0:T(8,128)(2,1)S(1)}, u32[]{:S(2)}, u32[]{:S(2)}) collective-permute-start(bf16[96,768]{1,0:T(8,128)(2,1)S(1)} %get-tuple-element.30), channel_id=1, source_target_pairs={{0,32},{1,225},{2,34},{3,227},{4,36},{5,229},{6,38},{7,231},{8,40}... | collective-permute-start | bytes 442376 | tf_op jit(solution)/shard_map/ppermute | solution.py:42
  46.9 12.6 %collective-permute-start.4 = (bf16[144,768]{1,0:T(8,128)(2,1)S(1)}, bf16[144,768]{1,0:T(8,128)(2,1)S(1)}, u32[]{:S(2)}, u32[]{:S(2)}) collective-permute-start(bf16[144,768]{1,0:T(8,128)(2,1)S(1)} %send.1.after_ref), channel_id=1, source_target_pairs={{0,32},{1,225},{2,34},{3,227},{4,36},{5,229},{6,38},{7,231},{8,40}... | collective-permute-start | bytes 663560 | tf_op jit(solution)/shard_map/ppermute | solution.py:42
  49.9 10.5 %collective-permute-start.6 = (bf16[144,768]{1,0:T(8,128)(2,1)S(1)}, bf16[144,768]{1,0:T(8,128)(2,1)S(1)}, u32[]{:S(2)}, u32[]{:S(2)}) collective-permute-start(bf16[144,768]{1,0:T(8,128)(2,1)S(1)} %pass.2), channel_id=1, source_target_pairs={{0,224},{1,33},{2,226},{3,35},{4,228},{5,37},{6,230},{7,39},{8,232... | collective-permute-start | bytes 663560 | tf_op jit(solution)/shard_map/ppermute | solution.py:42
  53.1 3.5 %collective-permute-start.8 = (bf16[48,768]{1,0:T(8,128)(2,1)S(1)}, bf16[48,768]{1,0:T(8,128)(2,1)S(1)}, u32[]{:S(2)}, u32[]{:S(2)}) collective-permute-start(bf16[48,768]{1,0:T(8,128)(2,1)S(1)} %pass.3), channel_id=1, source_target_pairs={{0,224},{1,33},{2,226},{3,35},{4,228},{5,37},{6,230},{7,39},{8,232... | collective-permute-start | bytes 221192 | tf_op jit(solution)/shard_map/ppermute | solution.py:42
  56.7 11.4 %collective-permute-start.9 = (bf16[48,768]{1,0:T(8,128)(2,1)S(1)}, bf16[48,768]{1,0:T(8,128)(2,1)S(1)}, u32[]{:S(2)}, u32[]{:S(2)}) collective-permute-start(bf16[48,768]{1,0:T(8,128)(2,1)S(1)} %far.1.after_ref), channel_id=1, source_target_pairs={{0,112},{1,177},{2,114},{3,179},{4,116},{5,181},{6,118},{7,183},{8... | collective-permute-start | bytes 221192 | tf_op jit(solution)/shard_map/ppermute | solution.py:42
  60.5 7.7 %collective-permute-start.10 = (bf16[48,768]{1,0:T(8,128)(2,1)S(1)}, bf16[48,768]{1,0:T(8,128)(2,1)S(1)}, u32[]{:S(2)}, u32[]{:S(2)}) collective-permute-start(bf16[48,768]{1,0:T(8,128)(2,1)S(1)} %get-tuple-element.31), channel_id=1, source_target_pairs={{0,96},{1,161},{2,98},{3,163},{4,100},{5,165},{6,102},{7,167},{8,1... | collective-permute-start | bytes 221192 | tf_op jit(solution)/shard_map/ppermute | solution.py:42
  65.0 5.6 %collective-permute-start.11 = (bf16[48,768]{1,0:T(8,128)(2,1)S(1)}, bf16[48,768]{1,0:T(8,128)(2,1)S(1)}, u32[]{:S(2)}, u32[]{:S(2)}) collective-permute-start(bf16[48,768]{1,0:T(8,128)(2,1)S(1)} %get-tuple-element.32), channel_id=1, source_target_pairs={{0,16},{1,17},{2,18},{3,19},{4,20},{5,21},{6,22},{7,23},{8,24},{9,... | collective-permute-start | bytes 221192 | tf_op jit(solution)/shard_map/ppermute | solution.py:42
